TPU v7x, 512 devices: a whole 4x4x16 slice. The times are simulated.
512 devices in a mesh: grid: 8 (over x, core), samp: 64 (over z, y).
Axes of the slice: x: 4, y: 4, z: 16, core: 2. Of those that a mesh axis runs over, the one named last changes fastest.
Arguments:
- summary: bfloat16 [131072, 1024], P('samp'), may hold values from -10 to 10
- kernel: bfloat16 [1024, 4096], P(None, 'grid'), may hold values from -1 to 1
- grid_offset: float32 [4096], P('grid'), may hold values from -130 to 130
- log_prior: float32 [131072], P('samp'), may hold values from -6 to 6
- tile_event: int32 [1024], P('samp'), may hold values from 0 to 63, as said below
- tile_live: int32 [1024], P('samp'), may hold values from 2 to 128
Outputs:
- log_evidence: float32 [64, 4096], P('samp', 'grid')
- ess_fraction: float32 [64, 4096], P('samp', 'grid')
- log_posterior: float32 [4096], P('grid')
Inputs may be any that keep to these rules, and one draw needn't show every extreme that they name: `tile_event`: every event owns at least one tile.
All inputs are finite; a program needn't handle non-finite values.
Results may differ from a plain program's by a relative error of at most 0.0003.
Values sent between devices are 32-bit elements; how exact they have to be, the bound alone decides.
A program may use at most 64 MiB of HBM per device.

v0:
```python
import jax
import jax.numpy as jnp
from jax import lax
from jax.sharding import PartitionSpec as P

EVENTS = 64


def sent_together(arrays, axis, split_dim, concat_dim, along):
    both = jnp.concatenate(arrays, axis=along)
    filled, at, gathered = (
        lax.all_to_all(both, axis, split_axis=split_dim, concat_axis=concat_dim, tiled=True),
        0,
        [],
    )
    for a in arrays:
        gathered.append(lax.slice_in_dim(filled, at, at + a.shape[along], axis=along))
        at += a.shape[along]
    return tuple(gathered)


def from_everyone(value, axis):
    copies = jnp.broadcast_to(value, (lax.axis_size(axis), *value.shape))
    return lax.all_to_all(copies, axis, split_axis=0, concat_axis=0, tiled=True)


def over_copies(value, axis):
    everything = from_everyone(value, axis)
    return jnp.sum(everything, axis=0)


def all_in_one(value, axis):
    leaves = jax.tree.leaves(value)
    sequence = sorted(range(len(leaves)), key=lambda k: -leaves[k].size)
    width = (1, *leaves[sequence[0]].shape)[-1]
    lines = [
        jnp.pad(leaves[k].reshape(-1), (0, -leaves[k].size % width)).reshape(-1, width)
        for k in sequence
    ]
    both, at, found = (from_everyone(jnp.concatenate(lines), axis), 0, {})
    for k, line in zip(sequence, lines):
        slab = both[:, at : at + len(line)].reshape(len(both), -1)
        found[k] = slab[:, : leaves[k].size].reshape(-1, *leaves[k].shape)
        at += len(line)
    numbers = iter(range(len(leaves)))
    return jax.tree.map(lambda _: found[next(numbers)], value)


def joined_by_halves(pieces, combine):
    while len(jax.tree.leaves(pieces)[0]) > 1:
        pieces = jax.vmap(combine)(
            *(jax.tree.map(lambda part: part[side::2], pieces) for side in (0, 1))
        )
    return jax.tree.map(lambda part: part[0], pieces)


def joined_all(value, axis, combine):
    pieces = all_in_one(value, axis)
    return joined_by_halves(pieces, combine)


def merge_grid(earlier, later):
    top_new = jnp.maximum(earlier[0], later[0])
    return (
        top_new,
        earlier[1] * jnp.exp(earlier[0] - top_new) + later[1] * jnp.exp(later[0] - top_new),
    )


def body(summary, kernel, grid_offset, log_prior, tile_event, tile_live):
    row_count = summary.shape[0]
    grid_cols = kernel.shape[1]
    tile_count = tile_event.shape[0]
    tile_rows = row_count // tile_count
    scores = jnp.dot(summary, kernel, preferred_element_type=jnp.float32)
    scores = scores + grid_offset[None, :] - log_prior[:, None]
    scores = scores.reshape(tile_count, tile_rows, grid_cols)
    is_live = lax.broadcasted_iota(jnp.int32, (tile_count, tile_rows), 1) < tile_live[:, None]
    masked = jnp.where(is_live[:, :, None], scores, jnp.float32(-1e30))
    tile_max = jnp.max(masked, axis=1)
    shifted = jnp.exp(masked - tile_max[:, None, :])
    tile_first = jnp.sum(shifted, axis=1)
    tile_second = jnp.sum(shifted * shifted, axis=1)
    member = tile_event[None, :] == lax.broadcasted_iota(jnp.int32, (EVENTS, tile_count), 0)
    local_peak = jnp.max(
        jnp.where(member[:, :, None], tile_max[None, :, :], jnp.float32(-1e30)), axis=1
    )
    live_count = jnp.sum(jnp.where(member, tile_live[None, :], 0), axis=1).astype(jnp.float32)
    factor = jnp.exp(tile_max - local_peak[tile_event])
    member_float = member.astype(jnp.float32)
    local_first = jnp.dot(member_float, tile_first * factor, precision=lax.Precision.HIGHEST)
    local_second = jnp.dot(
        member_float, tile_second * factor * factor, precision=lax.Precision.HIGHEST
    )
    got_peak, got_first, got_second, got_count = sent_together(
        (
            local_peak[:, None, :],
            local_first[:, None, :],
            local_second[:, None, :],
            live_count[:, None, None],
        ),
        "samp",
        0,
        1,
        2,
    )
    event_peak = jnp.max(got_peak, axis=1)
    rescale = jnp.exp(got_peak - event_peak[:, None, :])
    first_sum = jnp.sum(got_first * rescale, axis=1)
    second_sum = jnp.sum(got_second * rescale * rescale, axis=1)
    total_live = jnp.sum(got_count[:, :, 0], axis=1)
    log_evidence = event_peak + jnp.log(first_sum) - jnp.log(total_live)[:, None]
    ess_fraction = first_sum * first_sum / (second_sum * total_live[:, None])
    loglik = over_copies(jnp.sum(log_evidence, axis=0), "samp") / jnp.float32(EVENTS)
    local_top = jnp.max(loglik)
    grid_top, grid_mass = joined_all(
        (local_top, jnp.sum(jnp.exp(loglik - local_top))), "grid", merge_grid
    )
    log_posterior = loglik - (grid_top + jnp.log(grid_mass))
    return (log_evidence, ess_fraction, log_posterior)


def solution(mesh):
    in_specs = (P("samp", None), P(None, "grid"), P("grid"), P("samp"), P("samp"), P("samp"))
    out_specs = (P("samp", "grid"), P("samp", "grid"), P("grid"))
    return jax.shard_map(body, mesh=mesh, in_specs=in_specs, out_specs=out_specs, check_vma=False)
```

profile of v0, /device:TPU:1, one launch (start us, length us, event | category | flops | bytes accessed | tf_op | source)
XLA Modules:
  0.0 105.2 jit_solution(10106394739972559353)
XLA Ops:
  0.6 0.8 iota_compare_fusion.1
  1.5 0.7 compare_select_fusion
  2.1 0.7 iota_compare_fusion
  2.8 0.8 select_reduce_fusion.2
  3.6 0.1 copy.19
  3.7 4.6 %select_reduce_fusion = (f32[16,512]{1,0:T(8,128)S(1)}, f32[2048,512]{1,0:T(8,128)S(1)}) fusion(f32[2048]{0:T(1024)} %param.9, f32[512]{0:T(512)} %param.8, pred[16,128]{1,0:T(8,128)(4,1)S(1)} %iota_compare_fusion, bf16[2048,1024]{1,0:T(8,128)(2,1)} %param.6, bf16[1024,512]{1,0:T(8,128)(2,1)S(1)} %copy-done), kind=kOutput, calls=%fused_computation.4 | convolution fusion | flops 2151669760 | bytes 9482240 | tf_op jit(solution)/shard_map/dot_general | solution.py:75
  8.4 1.8 %fusion = (f32[16,512]{1,0:T(8,128)S(1)}, f32[16,512]{1,0:T(8,128)S(1)}) fusion(f32[2048,512]{1,0:T(8,128)S(1)} %get-tuple-element.20, f32[16,512]{1,0:T(8,128)S(1)} %get-tuple-element.19, f32[2048]{0:T(1024)S(1)} %copy-done.1, f32[512]{0:T(512)S(1)} %copy-done.2, pred[16,128]{1,0:T(8,128)(4,1)S(1)} %iota_compare_fusion), kind=kLoop, calls=%fused_computation.5 | loop fusion | flops 7323648 | bytes 4304896 | tf_op jit(solution)/shard_map/reduce_sum | solution.py:82
  10.2 0.5 select_reduce_fusion.1
  10.7 0.6 gather_fusion
  11.3 0.3 convolution_bitcast_fusion.1
  11.6 0.3 convolution_bitcast_fusion
  12.0 0.1 copy.20
  12.1 0.4 copy.21
  12.5 45.1 %all_to_all.23 = f32[64,1,1537]{2,1,0:T(1,128)S(1)} all-to-all(f32[64,1,1537]{2,1,0:T(1,128)S(1)} %copy.21), channel_id=1, replica_groups=mesh['grid'=8,'samp'=64] {'samp'}, dimensions={0} | all-to-all | bytes 786944 | tf_op jit(solution)/shard_map/all_to_all | solution.py:12
  57.6 0.1 slice_reduce_fusion
  57.8 0.7 slice_reduce_fusion.1
  58.4 0.4 fusion.2
  59.5 1.2 %multiply_divide_fusion = (f32[512]{0:T(512)}, f32[512]{0:T(512)S(1)}) fusion(f32[512]{0:T(512)S(1)} %get-tuple-element.5, f32[512]{0:T(512)S(1)} %get-tuple-element.6, f32[]{:T(128)} %slice_reduce_fusion.1, f32[]{:T(128)S(6)} %log.22, f32[512]{0:T(512)S(1)} %slice_reduce_fusion), kind=kLoop, calls=%fused_computation.30 | loop fusion | flops 2560 | bytes 10248 | tf_op jit(solution)/shard_map/div | solution.py:113
  60.8 22.5 %all_to_all.24 = f32[64,1,512]{2,1,0:T(1,128)S(1)} all-to-all(f32[64,1,512]{2,1,0:T(1,128)S(1)} %broadcast_in_dim.86), channel_id=1, replica_groups=mesh['grid'=8,'samp'=64] {'samp'}, dimensions={0} | all-to-all | bytes 262144 | tf_op jit(solution)/shard_map/all_to_all | solution.py:24
  83.3 0.1 reduce_sum.82
  83.4 0.6 multiply_reduce_fusion.1
  84.0 1.3 %exponential_reduce_fusion = f32[]{:T(128)} fusion(f32[512]{0:T(512)S(1)} %reduce_sum.82, f32[]{:T(128)} %multiply_reduce_fusion.1), kind=kLoop, calls=%fused_computation.29 | loop fusion | flops 1535 | bytes 2056 | tf_op jit(solution)/shard_map/reduce_sum | solution.py:117
  85.4 1.4 %maximum_bitcast_fusion = f32[2]{0:T(128)S(1)} fusion(f32[1,1]{0,1:T(1,128)} %bitcast.9, f32[1,1]{0,1:T(1,128)} %bitcast.8), kind=kLoop, calls=%fused_computation.34 | loop fusion | flops 2 | bytes 16 | tf_op jit(solution)/shard_map/concatenate | solution.py:40
  86.8 12.3 %all_to_all.25 = f32[8,2,1]{1,2,0:T(1,128)S(1)} all-to-all(f32[8,2,1]{1,2,0:T(1,128)S(1)} %broadcast_in_dim.87), channel_id=1, replica_groups=mesh['grid'=8,'samp'=64] {'grid'}, dimensions={0} | all-to-all | bytes 128 | tf_op jit(solution)/shard_map/all_to_all | solution.py:24
  99.1 0.2 slice_reduce_fusion.2
  99.3 0.1 slice.63
  99.4 0.1 slice.64
  99.5 0.1 slice.70
  99.6 0.1 slice.71
  99.7 0.1 slice.65
  100.1 0.6 fusion.6
  104.6 0.6 multiply_subtract_fusion
  (20 shorter events, 0.5 us)
Async XLA Ops:
  0.6 3.1 %copy-start = (bf16[1024,512]{1,0:T(8,128)(2,1)S(1)}, bf16[1024,512]{1,0:T(8,128)(2,1)}, u32[]{:S(2)}) copy-start(bf16[1024,512]{1,0:T(8,128)(2,1)} %param.7) | copy-start | bytes 3145732
  3.7 4.7 %copy-start.1 = (f32[2048]{0:T(1024)S(1)}, f32[2048]{0:T(1024)}, u32[]{:S(2)}) copy-start(f32[2048]{0:T(1024)} %param.9) | copy-start | bytes 24580
  3.7 4.7 %copy-start.2 = (f32[512]{0:T(512)S(1)}, f32[512]{0:T(512)}, u32[]{:S(2)}) copy-start(f32[512]{0:T(512)} %param.8) | copy-start | bytes 6148
  8.4 2.9 %copy-start.4 = (s32[16]{0:T(128)S(1)}, s32[16]{0:T(128)}, u32[]{:S(2)}) copy-start(s32[16]{0:T(128)} %param.10) | copy-start | bytes 196
  60.7 44.4 %copy-start.3 = (f32[512]{0:T(512)}, f32[512]{0:T(512)S(1)}, u32[]{:S(2)}) copy-start(f32[512]{0:T(512)S(1)} %get-tuple-element.14) | copy-start | bytes 6148
where the time goes:
time: 106 us; the launch traced here: 105 us
  blocking collectives  79.9 us (75%)
  other arithmetic  11.7 us (11%)
  between operations  5.33 us (5%)
  matrix products  5.25 us (5%)
  local copies, waits for them, and re-layouts  2.9 us (3%)
    all_to_all x1, blocking collectives, sent_together(): lax.all_to_all(both, axis, split_axis=split_dim, concat_axis=concat_dim,...  45.1 us
    all_to_all x2, blocking collectives, from_everyone(): return lax.all_to_all(copies, axis, split_axis=0, concat_axis=0, tiled=True)  34.8 us
    dot_general x1, matrix products, body(): scores = jnp.dot(summary, kernel, preferred_element_type=jnp.float32)  4.61 us

commit v1 on v0

v1 whole, which is shorter than its diff:
```python
import jax
import jax.numpy as jnp
from jax import lax
from jax.experimental import pallas as pl
from jax.experimental.pallas import tpu as pltpu
from jax.sharding import PartitionSpec as P

EVENTS = 64
NX, NC, NY, NZ = 4, 2, 4, 16
NG = NX * NC
TILE = 128
LANE = 128
NJ = 4
TILES = 16
GROUPS = 4
PER = TILES // GROUPS
BIG = -1e30
LOG2E = 1.4426950408889634
MESH = pl.DeviceIdType.MESH


def at_device(grid, samp):
    return (grid, samp)


def kernel(
    summary, weight, prior, offset, event, live,
    evidence_out, ess_out, posterior_out,
    x_buf, w_buf, scores, prior_buf, offset_buf,
    yid, yst, zsend, zrecv, csend, crecv, lbuf, vbuf,
    in_sem, y_send, y_recv, id_send, id_recv, z_send, z_recv, c_send, c_recv,
    l_send, l_recv, v_send, v_recv,
):
    gi, si = lax.axis_index("grid"), lax.axis_index("samp")
    x, c = gi // NC, lax.rem(gi, NC)
    z, y = si // NY, lax.rem(si, NY)
    rows = x_buf.shape[0]
    chunk = rows // GROUPS

    y_peers = [(gi, z * NY + lax.rem(y + d, NY)) for d in range(1, NY)]
    z_index = [lax.rem(z + d, NZ) for d in range(1, NZ)]
    z_peers = [(gi, zi * NY + y) for zi in z_index]
    v_peers = []
    for dx in range(NX):
        for dc in range(NC):
            for dy in range(NY):
                if dx or dc or dy:
                    grid = lax.rem(x + dx, NX) * NC + lax.rem(c + dc, NC)
                    v_peers.append((grid, z * NY + lax.rem(y + dy, NY)))

    copies = [
        pltpu.make_async_copy(weight, w_buf, in_sem.at[0]),
        pltpu.make_async_copy(prior, prior_buf, in_sem.at[1]),
        pltpu.make_async_copy(offset, offset_buf, in_sem.at[2]),
    ]
    for g in range(GROUPS):
        part = pl.ds(g * chunk, chunk)
        copies.append(pltpu.make_async_copy(summary.at[part], x_buf.at[part], in_sem.at[3 + g]))
    for copy in copies:
        copy.start()

    barrier = pltpu.get_barrier_semaphore()
    greeted = z_peers + v_peers
    for peer in greeted:
        pl.semaphore_signal(barrier, inc=1, device_id=peer, device_id_type=MESH)

    for t in range(TILES):
        yid[y, 0, t : t + 1, :] = jnp.full((1, LANE), event[t].astype(jnp.float32))
        yid[y, 1, t : t + 1, :] = jnp.full((1, LANE), live[t].astype(jnp.float32))

    lane = lax.broadcasted_iota(jnp.int32, (1, LANE), 1)

    def dot(g):
        copies[3 + g].wait()
        scores[g % 2] = jnp.dot(
            x_buf[g * chunk : (g + 1) * chunk, :], w_buf[...], preferred_element_type=jnp.float32
        )

    def stats(g):
        for i in range(PER):
            t = g * PER + i
            add = jnp.where(lane < live[t], -prior_buf[t : t + 1, :], BIG)
            add = jnp.transpose(jnp.broadcast_to(add, (LANE, LANE)))
            for j in range(NJ):
                v = scores[g % 2, i * TILE : (i + 1) * TILE, j * LANE : (j + 1) * LANE] + add
                top = jnp.max(v, axis=0, keepdims=True)
                p = jnp.exp2((v - top) * LOG2E)
                first = jnp.sum(p, axis=0, keepdims=True)
                second = jnp.sum(p * p, axis=0, keepdims=True)
                at = i * NJ + j
                yst[g, y, 0, at : at + 1, :] = top + jnp.log(first)
                yst[g, y, 1, at : at + 1, :] = second / (first * first)

    copies[0].wait()
    copies[1].wait()
    dot(0)
    for g in range(1, GROUPS):
        dot(g)
        stats(g - 1)
    stats(GROUPS - 1)

    pl.semaphore_wait(barrier, len(greeted))

    sends = []

    def remote(src, dst, send_sem, recv_sem, peer):
        copy = pltpu.make_async_remote_copy(
            src_ref=src, dst_ref=dst, send_sem=send_sem, recv_sem=recv_sem,
            device_id=peer, device_id_type=MESH,
        )
        copy.start()

    def arrived(ref, send_sem, recv_sem):
        copy = pltpu.make_async_remote_copy(
            src_ref=ref, dst_ref=ref, send_sem=send_sem, recv_sem=recv_sem,
            device_id=y_peers[0], device_id_type=MESH,
        )
        copy.wait_recv()
        sends.append(copy)

    for peer in y_peers:
        remote(yid.at[y], yid.at[y], id_send, id_recv, peer)
    for g in range(GROUPS):
        for peer in y_peers:
            remote(yst.at[g, y], yst.at[g, y], y_send.at[g], y_recv.at[g], peer)

    arrived(yid.at[pl.ds(0, NY - 1)], id_send, id_recv)
    mine = lax.broadcasted_iota(jnp.int32, (NZ, LANE), 0) * NY + y
    mine = mine.astype(jnp.float32)

    def member(s, t):
        return jnp.broadcast_to(yid[s, 0, t : t + 1, :], (NZ, LANE)) == mine

    count = jnp.zeros((NZ, LANE), jnp.float32)
    for s in range(NY):
        for t in range(TILES):
            count += jnp.where(member(s, t), yid[s, 1, t : t + 1, :], 0.0)
    for k in range(NZ):
        csend[k] = count[k : k + 1, :]
    crecv[z] = csend[z]
    for zi, peer in zip(z_index, z_peers):
        remote(csend.at[zi], crecv.at[z], c_send, c_recv, peer)

    for g in range(GROUPS):
        arrived(yst.at[g, pl.ds(0, NY - 1)], y_send.at[g], y_recv.at[g])
    order = [(s, g, i) for g in range(GROUPS) for s in range(NY) for i in range(PER)]
    for j in range(NJ):
        top = jnp.full((NZ, LANE), BIG, jnp.float32)
        for s, g, i in order:
            at = i * NJ + j
            row = yst[g, s, 0, at : at + 1, :]
            top = jnp.maximum(top, jnp.where(member(s, g * PER + i), row, BIG))
        first = jnp.zeros((NZ, LANE), jnp.float32)
        second = jnp.zeros((NZ, LANE), jnp.float32)
        for s, g, i in order:
            at = i * NJ + j
            row = jnp.where(member(s, g * PER + i), yst[g, s, 0, at : at + 1, :], BIG)
            w = jnp.exp2((row - top) * LOG2E)
            first += w
            second += w * w * yst[g, s, 1, at : at + 1, :]
        zsend[pl.ds(j, NZ, stride=8), :] = top + jnp.log(first)
        zsend[pl.ds(NJ + j, NZ, stride=8), :] = second / (first * first)

    def block(index):
        return pl.ds(pl.multiple_of(index * 8, 8), 8)

    for zi, peer in zip(z_index, z_peers):
        remote(zsend.at[block(zi)], zrecv.at[block(z)], z_send, z_recv, peer)
    zrecv[block(z), :] = zsend[block(z), :]

    arrived(crecv.at[pl.ds(0, NZ - 1)], c_send, c_recv)
    total = crecv[0]
    for k in range(1, NZ):
        total += crecv[k]
    copies[2].wait()
    arrived(zrecv.at[pl.ds(0, 8 * (NZ - 1))], z_send, z_recv)
    top = zrecv[0:NJ, :]
    for k in range(1, NZ):
        top = jnp.maximum(top, zrecv[8 * k : 8 * k + NJ, :])
    first = jnp.zeros((NJ, LANE), jnp.float32)
    second = jnp.zeros((NJ, LANE), jnp.float32)
    for k in range(NZ):
        w = jnp.exp2((zrecv[8 * k : 8 * k + NJ, :] - top) * LOG2E)
        first += w
        second += w * w * zrecv[8 * k + NJ : 8 * k + 8, :]
    evidence = (top + jnp.log(first)) + offset_buf[...] - jnp.log(total)
    lbuf[z] = evidence
    for peer in z_peers:
        remote(lbuf.at[z], lbuf.at[z], l_send, l_recv, peer)
    evidence_out[...] = evidence
    ess_out[...] = first * first / (second * total)

    arrived(lbuf.at[pl.ds(0, NZ - 1)], l_send, l_recv)
    partial = lbuf[0]
    for k in range(1, NZ):
        partial += lbuf[k]
    vbuf[gi * NY + y] = partial
    for peer in v_peers:
        remote(vbuf.at[gi * NY + y], vbuf.at[gi * NY + y], v_send, v_recv, peer)
    arrived(vbuf.at[pl.ds(0, NG * NY - 1)], v_send, v_recv)

    def loglik(index):
        value = vbuf[index * NY]
        for k in range(1, NY):
            value += vbuf[index * NY + k]
        return value * (1.0 / EVENTS)

    lines = [loglik(k) for k in range(NG)]
    best = lines[0]
    for line in lines[1:]:
        best = jnp.maximum(best, line)
    best = jnp.max(best)
    mass = jnp.zeros((NJ, LANE), jnp.float32)
    for line in lines:
        mass += jnp.exp2((line - best) * LOG2E)
    mass = jnp.sum(mass)
    norm = best + jnp.log(jnp.full((NJ, LANE), mass))
    posterior_out[...] = loglik(gi) - norm

    for copy in sends:
        copy.wait_send()


def body(summary, weight, offset, prior, event, live):
    rows, bins = summary.shape
    cols = weight.shape[1]
    dma, vmem = pltpu.SemaphoreType.DMA, pltpu.VMEM
    f32 = jnp.float32
    small = jax.ShapeDtypeStruct((NJ, LANE), f32)
    hbm = pl.BlockSpec(memory_space=pltpu.HBM)
    smem = pl.BlockSpec(memory_space=pltpu.SMEM)
    outs = pl.pallas_call(
        kernel,
        name="reweight",
        out_shape=(small, small, small),
        in_specs=[hbm, hbm, hbm, hbm, smem, smem],
        out_specs=(pl.BlockSpec(memory_space=pltpu.VMEM),) * 3,
        scratch_shapes=[
            vmem((rows, bins), jnp.bfloat16),
            vmem((bins, cols), jnp.bfloat16),
            vmem((2, rows // GROUPS, cols), f32),
            vmem((TILES, LANE), f32),
            vmem((NJ, LANE), f32),
            vmem((NY, 2, TILES, LANE), f32),
            vmem((GROUPS, NY, 2, PER * NJ, LANE), f32),
            vmem((NZ * 8, LANE), f32),
            vmem((NZ * 8, LANE), f32),
            vmem((NZ, 1, LANE), f32),
            vmem((NZ, 1, LANE), f32),
            vmem((NZ, NJ, LANE), f32),
            vmem((NG * NY, NJ, LANE), f32),
            dma((3 + GROUPS,)),
            dma((GROUPS,)),
            dma((GROUPS,)),
            dma, dma, dma, dma, dma, dma, dma, dma, dma, dma,
        ],
        compiler_params=pltpu.CompilerParams(
            collective_id=0, has_side_effects=True, vmem_limit_bytes=32 * 1024 * 1024
        ),
        cost_estimate=pl.CostEstimate(
            flops=2 * rows * bins * cols, bytes_accessed=2 * rows * bins, transcendentals=rows * cols
        ),
    )(summary, weight, prior.reshape(TILES, LANE), offset.reshape(NJ, LANE), event, live)
    evidence, ess, posterior = outs
    return evidence.reshape(1, cols), ess.reshape(1, cols), posterior.reshape(cols)


def solution(mesh):
    in_specs = (P("samp", None), P(None, "grid"), P("grid"), P("samp"), P("samp"), P("samp"))
    out_specs = (P("samp", "grid"), P("samp", "grid"), P("grid"))
    return jax.shard_map(body, mesh=mesh, in_specs=in_specs, out_specs=out_specs, check_vma=False)
```

time: 106 us -> 55 us (0.52)
  blocking collectives: 79.9 us -> 0 us
  Pallas kernels: 0 us -> 46.2 us
  other arithmetic: 11.7 us -> 0 us
  matrix products: 5.25 us -> 0 us
  local copies, waits for them, and re-layouts: 2.9 us -> 7.83 us
  between operations: 5.33 us -> 0.65 us
    all_to_all x3 -> x0, blocking collectives: 79.9 us -> none  [the longest x1 45.1 us: sent_together(): lax.all_to_all(both, axis, split_axis=split_dim, concat_axis=concat_dim,...]
    pallas_call x0 -> x1, Pallas kernels: none -> 46.2 us  [body(): pl.pallas_call(kernel, name='reweight', out_shape=(small, small, small),...]
    unnamed x10 -> x15, local copies, waits for them, and re-layouts: 0.03 us -> 7.83 us
    dot_general x3 -> x0, matrix products: 5.25 us -> none  [the longest x1 4.61 us: body(): scores = jnp.dot(summary, kernel, preferred_element_type=jnp.float32)]
    reduce_sum x6 -> x0, other arithmetic: 5.04 us -> none  [the longest x1 1.81 us: body(): tile_first = jnp.sum(shifted, axis=1)]
    slice x10 -> x0, local copies, waits for them, and re-layouts: 1.58 us -> none  [the longest x9 1.37 us: joined_by_halves(): part[side::2]]
    concatenate x2 -> x0, other arithmetic: 1.44 us -> none  [the longest x1 1.41 us: all_in_one(): both, at, found = (from_everyone(jnp.concatenate(lines), axis), 0, {})]
    div x1 -> x0, other arithmetic: 1.23 us -> none  [body(): ess_fraction = first_sum * first_sum / (second_sum * total_live[:, None])]
where the time goes in v1:
time: 55 us; the launch traced here: 54.7 us
  Pallas kernels  46.2 us (84%)
  local copies, waits for them, and re-layouts  7.83 us (14%)
  between operations  0.65 us (1%)
    pallas_call x1, Pallas kernels, body(): pl.pallas_call(kernel, name='reweight', out_shape=(small, small, small),...  46.2 us
    unnamed x15, local copies, waits for them, and re-layouts  7.83 us

profile of v1, /device:TPU:1, one launch (start us, length us, event | category | flops | bytes accessed | tf_op | source)
XLA Modules:
  0.0 54.7 jit_solution(17176185040938518495)
XLA Ops:
  0.6 0.0 copy-start
  0.6 2.2 %copy-done = bf16[2048,1024]{1,0:T(8,128)(2,1)S(1)} copy-done((bf16[2048,1024]{1,0:T(8,128)(2,1)S(1)}, bf16[2048,1024]{1,0:T(8,128)(2,1)}, u32[]{:S(2)}) %copy-start) | copy-done | bytes 4194328
  2.8 0.0 copy-start.1
  2.8 1.2 %copy-done.1 = bf16[1024,512]{1,0:T(8,128)(2,1)S(1)} copy-done((bf16[1024,512]{1,0:T(8,128)(2,1)S(1)}, bf16[1024,512]{1,0:T(8,128)(2,1)}, u32[]{:S(2)}) %copy-start.1) | copy-done | bytes 1048600
  4.0 0.0 copy-start.2
  4.0 0.7 %copy-done.2 = f32[2048]{0:T(1024)S(1)} copy-done((f32[2048]{0:T(1024)S(1)}, f32[2048]{0:T(1024)}, u32[]{:S(2)}) %copy-start.2) | copy-done | bytes 8216
  4.7 0.0 copy-start.3
  4.7 0.7 %copy-done.3 = f32[512]{0:T(512)S(1)} copy-done((f32[512]{0:T(512)S(1)}, f32[512]{0:T(512)}, u32[]{:S(2)}) %copy-start.3) | copy-done | bytes 2072
  5.4 0.0 copy-start.4
  5.4 0.7 %copy-done.4 = s32[16]{0:T(128)S(1)} copy-done((s32[16]{0:T(128)S(1)}, s32[16]{0:T(128)}, u32[]{:S(2)}) %copy-start.4) | copy-done | bytes 88
  6.1 0.0 copy-start.5
  6.1 0.7 %copy-done.5 = s32[16]{0:T(128)S(1)} copy-done((s32[16]{0:T(128)S(1)}, s32[16]{0:T(128)}, u32[]{:S(2)}) %copy-start.5) | copy-done | bytes 88
  6.7 46.2 %reweight.1 = (f32[4,128]{1,0:T(4,128)S(1)}, f32[4,128]{1,0:T(4,128)S(1)}, f32[4,128]{1,0:T(4,128)S(1)}) custom-call(bf16[2048,1024]{1,0:T(8,128)(2,1)S(1)} %copy-done, bf16[1024,512]{1,0:T(8,128)(2,1)S(1)} %copy-done.1, f32[16,128]{1,0:T(8,128)S(1)} %bitcast.8, f32[4,128]{1,0:T(4,128)S(1)} %bitcast.9, s32[16]{0:T(128)S(1)} %copy-done.4, s32[16]{0:T(128)S(1)} %copy-done.5), custom_call_target="tpu_custom_call" | custom-call | flops 2147483648 | bytes 4194304 | tf_op jit(solution)/shard_map/reweight/pallas_call | solution.py:232
  53.0 0.6 %copy.12 = f32[1,512]{1,0:T(1,128)} copy(f32[1,512]{1,0:T(1,128)S(1)} %bitcast.7) | data formatting | bytes 4096
  53.6 0.6 %copy.13 = f32[1,512]{1,0:T(1,128)} copy(f32[1,512]{1,0:T(1,128)S(1)} %bitcast.6) | data formatting | bytes 4096
  54.1 0.6 %copy.14 = f32[512]{0:T(512)} copy(f32[512]{0:T(512)S(1)} %bitcast.5) | data formatting | bytes 4096
Async XLA Ops:
  0.6 2.2 %copy-start = (bf16[2048,1024]{1,0:T(8,128)(2,1)S(1)}, bf16[2048,1024]{1,0:T(8,128)(2,1)}, u32[]{:S(2)}) copy-start(bf16[2048,1024]{1,0:T(8,128)(2,1)} %summary.1) | copy-start | bytes 12582916
  2.8 1.2 %copy-start.1 = (bf16[1024,512]{1,0:T(8,128)(2,1)S(1)}, bf16[1024,512]{1,0:T(8,128)(2,1)}, u32[]{:S(2)}) copy-start(bf16[1024,512]{1,0:T(8,128)(2,1)} %weight.1) | copy-start | bytes 3145732
  4.0 0.7 %copy-start.2 = (f32[2048]{0:T(1024)S(1)}, f32[2048]{0:T(1024)}, u32[]{:S(2)}) copy-start(f32[2048]{0:T(1024)} %param.9) | copy-start | bytes 24580
  4.7 0.7 %copy-start.3 = (f32[512]{0:T(512)S(1)}, f32[512]{0:T(512)}, u32[]{:S(2)}) copy-start(f32[512]{0:T(512)} %param.8) | copy-start | bytes 6148
  5.4 0.7 %copy-start.4 = (s32[16]{0:T(128)S(1)}, s32[16]{0:T(128)}, u32[]{:S(2)}) copy-start(s32[16]{0:T(128)} %event.1) | copy-start | bytes 196
  6.1 0.7 %copy-start.5 = (s32[16]{0:T(128)S(1)}, s32[16]{0:T(128)}, u32[]{:S(2)}) copy-start(s32[16]{0:T(128)} %live.1) | copy-start | bytes 196

commit v2 on v1

--- a/solution.py
+++ b/solution.py
@@ -17,6 +17,7 @@
 BIG = -1e30
 LOG2E = 1.4426950408889634
 MESH = pl.DeviceIdType.MESH
+RELAY = (1, 2, 4)
 
 
 def at_device(grid, samp):
@@ -27,9 +28,9 @@
     summary, weight, prior, offset, event, live,
     evidence_out, ess_out, posterior_out,
     x_buf, w_buf, scores, prior_buf, offset_buf,
-    yid, yst, zsend, zrecv, csend, crecv, lbuf, vbuf,
+    yid, yst, held, zsend, zrecv, csend, crecv, lbuf, vbuf,
     in_sem, y_send, y_recv, id_send, id_recv, z_send, z_recv, c_send, c_recv,
-    l_send, l_recv, v_send, v_recv,
+    l_send, l_recv, v_send, v_recv, known,
 ):
     gi, si = lax.axis_index("grid"), lax.axis_index("samp")
     x, c = gi // NC, lax.rem(gi, NC)
@@ -59,10 +60,25 @@
     for copy in copies:
         copy.start()
 
+    def beside(d):
+        return [(gi, lax.rem(z + k, NZ) * NY + y) for k in (d, NZ - d)]
+
+    grid_peers = []
+    for dx in range(NX):
+        for dc in range(NC):
+            if dx or dc:
+                grid_peers.append((lax.rem(x + dx, NX) * NC + lax.rem(c + dc, NC), si))
+    near = y_peers + grid_peers + beside(1)
     barrier = pltpu.get_barrier_semaphore()
-    greeted = z_peers + v_peers
-    for peer in greeted:
+    for peer in near:
         pl.semaphore_signal(barrier, inc=1, device_id=peer, device_id_type=MESH)
+
+    def tell(k):
+        for peer in beside(RELAY[k]):
+            pl.semaphore_signal(known.at[k], inc=1, device_id=peer, device_id_type=MESH)
+
+    def heard(k):
+        pl.semaphore_wait(known.at[k], 2)
 
     for t in range(TILES):
         yid[y, 0, t : t + 1, :] = jnp.full((1, LANE), event[t].astype(jnp.float32))
@@ -91,16 +107,6 @@
                 yst[g, y, 0, at : at + 1, :] = top + jnp.log(first)
                 yst[g, y, 1, at : at + 1, :] = second / (first * first)
 
-    copies[0].wait()
-    copies[1].wait()
-    dot(0)
-    for g in range(1, GROUPS):
-        dot(g)
-        stats(g - 1)
-    stats(GROUPS - 1)
-
-    pl.semaphore_wait(barrier, len(greeted))
-
     sends = []
 
     def remote(src, dst, send_sem, recv_sem, peer):
@@ -118,11 +124,31 @@
         copy.wait_recv()
         sends.append(copy)
 
+    def send_stats(g):
+        for peer in y_peers:
+            remote(yst.at[g, y], yst.at[g, y], y_send.at[g], y_recv.at[g], peer)
+
+    def got_stats(g):
+        arrived(yst.at[g, pl.ds(0, NY - 1)], y_send.at[g], y_recv.at[g])
+
+    pl.semaphore_wait(barrier, len(near))
+    tell(0)
     for peer in y_peers:
         remote(yid.at[y], yid.at[y], id_send, id_recv, peer)
-    for g in range(GROUPS):
-        for peer in y_peers:
-            remote(yst.at[g, y], yst.at[g, y], y_send.at[g], y_recv.at[g], peer)
+    copies[0].wait()
+    copies[1].wait()
+    dot(0)
+    for g in range(1, GROUPS):
+        dot(g)
+        stats(g - 1)
+        send_stats(g - 1)
+        if g == 1:
+            heard(0)
+            tell(1)
+    stats(GROUPS - 1)
+    send_stats(GROUPS - 1)
+    heard(1)
+    tell(2)
 
     arrived(yid.at[pl.ds(0, NY - 1)], id_send, id_recv)
     mine = lax.broadcasted_iota(jnp.int32, (NZ, LANE), 0) * NY + y
@@ -138,28 +164,42 @@
     for k in range(NZ):
         csend[k] = count[k : k + 1, :]
     crecv[z] = csend[z]
+
+    def rows_of(groups):
+        return [(s, g, i) for g in groups for s in range(NY) for i in range(PER)]
+
+    def chosen(j, s, g, i):
+        at = i * NJ + j
+        return jnp.where(member(s, g * PER + i), yst[g, s, 0, at : at + 1, :], BIG)
+
+    def merged(j, order, top, first, second):
+        high = top
+        for entry in order:
+            high = jnp.maximum(high, chosen(j, *entry))
+        keep = jnp.exp2((top - high) * LOG2E)
+        first, second = first * keep, second * (keep * keep)
+        for s, g, i in order:
+            at = i * NJ + j
+            w = jnp.exp2((chosen(j, s, g, i) - high) * LOG2E)
+            first += w
+            second += w * w * yst[g, s, 1, at : at + 1, :]
+        return high, first, second
+
+    early, late = rows_of(range(GROUPS - 1)), rows_of([GROUPS - 1])
+    for g in range(GROUPS - 1):
+        got_stats(g)
+    zero = jnp.zeros((NZ, LANE), jnp.float32)
+    for j in range(NJ):
+        held[j, 0], held[j, 1], held[j, 2] = merged(j, early, zero + BIG, zero, zero)
+    got_stats(GROUPS - 1)
+    for j in range(NJ):
+        top, first, second = merged(j, late, held[j, 0], held[j, 1], held[j, 2])
+        zsend[pl.ds(j, NZ, stride=8), :] = top + jnp.log(first)
+        zsend[pl.ds(NJ + j, NZ, stride=8), :] = second / (first * first)
+
+    heard(2)
     for zi, peer in zip(z_index, z_peers):
         remote(csend.at[zi], crecv.at[z], c_send, c_recv, peer)
-
-    for g in range(GROUPS):
-        arrived(yst.at[g, pl.ds(0, NY - 1)], y_send.at[g], y_recv.at[g])
-    order = [(s, g, i) for g in range(GROUPS) for s in range(NY) for i in range(PER)]
-    for j in range(NJ):
-        top = jnp.full((NZ, LANE), BIG, jnp.float32)
-        for s, g, i in order:
-            at = i * NJ + j
-            row = yst[g, s, 0, at : at + 1, :]
-            top = jnp.maximum(top, jnp.where(member(s, g * PER + i), row, BIG))
-        first = jnp.zeros((NZ, LANE), jnp.float32)
-        second = jnp.zeros((NZ, LANE), jnp.float32)
-        for s, g, i in order:
-            at = i * NJ + j
-            row = jnp.where(member(s, g * PER + i), yst[g, s, 0, at : at + 1, :], BIG)
-            w = jnp.exp2((row - top) * LOG2E)
-            first += w
-            second += w * w * yst[g, s, 1, at : at + 1, :]
-        zsend[pl.ds(j, NZ, stride=8), :] = top + jnp.log(first)
-        zsend[pl.ds(NJ + j, NZ, stride=8), :] = second / (first * first)
 
     def block(index):
         return pl.ds(pl.multiple_of(index * 8, 8), 8)
@@ -221,18 +261,28 @@
         copy.wait_send()
 
 
+def finish(evidence, ess, posterior, evidence_out, ess_out, posterior_out, sem):
+    pairs = ((evidence, evidence_out), (ess, ess_out), (posterior, posterior_out))
+    copies = [pltpu.make_async_copy(a, b, sem.at[k]) for k, (a, b) in enumerate(pairs)]
+    for copy in copies:
+        copy.start()
+    for copy in copies:
+        copy.wait()
+
+
 def body(summary, weight, offset, prior, event, live):
     rows, bins = summary.shape
     cols = weight.shape[1]
     dma, vmem = pltpu.SemaphoreType.DMA, pltpu.VMEM
     f32 = jnp.float32
     small = jax.ShapeDtypeStruct((NJ, LANE), f32)
+    kept = vmem((NJ, LANE), f32)
     hbm = pl.BlockSpec(memory_space=pltpu.HBM)
     smem = pl.BlockSpec(memory_space=pltpu.SMEM)
     outs = pl.pallas_call(
         kernel,
         name="reweight",
-        out_shape=(small, small, small),
+        out_shape=(kept, kept, kept),
         in_specs=[hbm, hbm, hbm, hbm, smem, smem],
         out_specs=(pl.BlockSpec(memory_space=pltpu.VMEM),) * 3,
         scratch_shapes=[
@@ -243,6 +293,7 @@
             vmem((NJ, LANE), f32),
             vmem((NY, 2, TILES, LANE), f32),
             vmem((GROUPS, NY, 2, PER * NJ, LANE), f32),
+            vmem((NJ, 3, NZ, LANE), f32),
             vmem((NZ * 8, LANE), f32),
             vmem((NZ * 8, LANE), f32),
             vmem((NZ, 1, LANE), f32),
@@ -253,6 +304,7 @@
             dma((GROUPS,)),
             dma((GROUPS,)),
             dma, dma, dma, dma, dma, dma, dma, dma, dma, dma,
+            pltpu.SemaphoreType.REGULAR((len(RELAY),)),
         ],
         compiler_params=pltpu.CompilerParams(
             collective_id=0, has_side_effects=True, vmem_limit_bytes=32 * 1024 * 1024
@@ -260,8 +312,20 @@
         cost_estimate=pl.CostEstimate(
             flops=2 * rows * bins * cols, bytes_accessed=2 * rows * bins, transcendentals=rows * cols
         ),
-    )(summary, weight, prior.reshape(TILES, LANE), offset.reshape(NJ, LANE), event, live)
-    evidence, ess, posterior = outs
+    )(*(
+        pltpu.with_memory_space_constraint(a, pltpu.HBM)
+        for a in (summary, weight, prior.reshape(TILES, LANE), offset.reshape(NJ, LANE), event, live)
+    ))
+    vm, any_space = pl.BlockSpec(memory_space=pltpu.VMEM), pl.BlockSpec(memory_space=pltpu.HBM)
+    evidence, ess, posterior = pl.pallas_call(
+        finish,
+        name="finish",
+        out_shape=(small, small, small),
+        in_specs=[vm, vm, vm],
+        out_specs=(any_space,) * 3,
+        scratch_shapes=[dma((3,))],
+        compiler_params=pltpu.CompilerParams(vmem_limit_bytes=1024 * 1024),
+    )(*outs)
     return evidence.reshape(1, cols), ess.reshape(1, cols), posterior.reshape(cols)
 
 

time: 55 us -> 44.1 us (0.80)
  local copies, waits for them, and re-layouts: 7.83 us -> 0 us
  Pallas kernels: 46.2 us -> 43.4 us
    unnamed x15 -> x0, local copies, waits for them, and re-layouts: 7.83 us -> none
    pallas_call x1 -> x2, Pallas kernels: 46.2 us -> 43.4 us  [the longest x1 42.8 us: body(): pl.pallas_call(kernel, name='reweight', out_shape=(kept, kept, kept), in_...]
where the time goes in v2:
time: 44.1 us; the launch traced here: 44 us
  Pallas kernels  43.4 us (98%)
  between operations  0.64 us (1%)
    pallas_call x1, Pallas kernels, body(): pl.pallas_call(kernel, name='reweight', out_shape=(kept, kept, kept), in_...  42.8 us

profile of v2, /device:TPU:1, one launch (start us, length us, event | category | flops | bytes accessed | tf_op | source)
XLA Modules:
  0.0 44.0 jit_solution(17128455160591579955)
XLA Ops:
  0.6 42.8 %reweight.1 = (f32[4,128]{1,0:T(4,128)S(1)}, f32[4,128]{1,0:T(4,128)S(1)}, f32[4,128]{1,0:T(4,128)S(1)}) custom-call(bf16[2048,1024]{1,0:T(8,128)(2,1)} %summary.1, bf16[1024,512]{1,0:T(8,128)(2,1)} %weight.1, f32[16,128]{1,0:T(8,128)} %bitcast.5, f32[4,128]{1,0:T(4,128)} %bitcast.6, s32[16]{0:T(128)} %event.1, s32[16]{0:T(128)} %live.1), custom_call_target="tpu_custom_call" | custom-call | flops 2147483648 | bytes 4194304 | tf_op jit(solution)/shard_map/reweight/pallas_call | solution.py:282
  43.4 0.6 %finish.1 = (f32[4,128]{1,0:T(4,128)}, f32[4,128]{1,0:T(4,128)}, f32[4,128]{1,0:T(4,128)}) custom-call(f32[4,128]{1,0:T(4,128)S(1)} %get-tuple-element.9.evidence, f32[4,128]{1,0:T(4,128)S(1)} %get-tuple-element.10.ess, f32[4,128]{1,0:T(4,128)S(1)} %get-tuple-element.11.posterior), custom_call_target="tpu_custom_call" | custom-call | tf_op jit(solution)/shard_map/finish/pallas_call | solution.py:320

commit v3 on v1

v3 whole, which is shorter than its diff:
```python
import jax
import jax.numpy as jnp
from jax import lax
from jax.experimental import pallas as pl
from jax.experimental.pallas import tpu as pltpu
from jax.sharding import PartitionSpec as P

EVENTS = 64
NX, NC, NY, NZ = 4, 2, 4, 16
NG = NX * NC
TILE = 128
LANE = 128
NJ = 4
TILES = 16
OWN = EVENTS // NZ
SIZES = (256, 512, 512, 512, 256)
AHEAD = 2
HOP = 4
BIG = -1e30
LOG2E = 1.4426950408889634
MESH = pl.DeviceIdType.MESH


def kernel(
    summary, weight, prior, offset, event_in, live_in,
    evidence_out, ess_out, posterior_out,
    x_buf, w_buf, scores, prior_buf, offset_buf, event, live,
    yid, ysend, yrecv, held, zsend, zrecv, crecv, lbuf, osend, orecv, vbuf,
    in_sem, x_sem, id_send, id_recv, y_send, y_recv, c_send, c_recv, z_send, z_recv,
    l_send, l_recv, o_send, o_recv, v_send, v_recv, known,
):
    gi, si = lax.axis_index("grid"), lax.axis_index("samp")
    x, c = gi // NC, lax.rem(gi, NC)
    z, y = si // NY, lax.rem(si, NY)

    starts = [sum(SIZES[:g]) for g in range(len(SIZES))]
    x_copies = []
    for g, (at, size) in enumerate(zip(starts, SIZES)):
        part = pl.ds(at, size)
        x_copies.append(pltpu.make_async_copy(summary.at[part], x_buf.at[part], x_sem.at[g]))
    pairs = (
        (weight, w_buf), (prior, prior_buf), (event_in, event), (live_in, live), (offset, offset_buf)
    )
    w_copy, *small_copies = [
        pltpu.make_async_copy(a, b, in_sem.at[k]) for k, (a, b) in enumerate(pairs)
    ]
    w_copy.start()
    for copy in x_copies[:AHEAD]:
        copy.start()
    for copy in small_copies:
        copy.start()

    y_index = [lax.rem(y + d, NY) for d in range(1, NY)]
    y_peers = [(gi, z * NY + k) for k in y_index]
    z_index = [lax.rem(z + d, NZ) for d in range(1, NZ)]
    z_peers = [(gi, k * NY + y) for k in z_index]
    grid_peers, v_peers = [], []
    for dx in range(NX):
        for dc in range(NC):
            grid = lax.rem(x + dx, NX) * NC + lax.rem(c + dc, NC)
            if dx or dc:
                grid_peers.append((grid, si))
            for dy in range(NY):
                if dx or dc or dy:
                    v_peers.append((grid, z * NY + lax.rem(y + dy, NY)))

    near = y_peers + grid_peers + [z_peers[d - 1] for k in range(1, HOP + 1) for d in (k, NZ - k)]
    barrier = pltpu.get_barrier_semaphore()
    for peer in near:
        pl.semaphore_signal(barrier, inc=1, device_id=peer, device_id_type=MESH)

    lane = lax.broadcasted_iota(jnp.int32, (1, LANE), 1)

    def dot(g):
        x_copies[g].wait()
        if g + AHEAD < len(SIZES):
            x_copies[g + AHEAD].start()
        scores[g % 2, : SIZES[g], :] = jnp.dot(
            x_buf[starts[g] : starts[g] + SIZES[g], :], w_buf[...],
            preferred_element_type=jnp.float32,
        )

    def stats(g):
        for i in range(SIZES[g] // TILE):
            t = starts[g] // TILE + i
            add = jnp.where(lane < live[t], -prior_buf[t : t + 1, :], BIG)
            add = jnp.transpose(jnp.broadcast_to(add, (LANE, LANE)))
            for j in range(NJ):
                v = scores[g % 2, i * TILE : (i + 1) * TILE, j * LANE : (j + 1) * LANE] + add
                top = jnp.max(v, axis=0, keepdims=True)
                p = jnp.exp2((v - top) * LOG2E)
                first = jnp.sum(p, axis=0, keepdims=True)
                second = jnp.sum(p * p, axis=0, keepdims=True)
                ysend[j, t, 0:1, :] = top + jnp.log(first)
                ysend[j, t, 1:2, :] = second / (first * first)

    sends = []

    def remote(src, dst, send_sem, recv_sem, peer):
        copy = pltpu.make_async_remote_copy(
            src_ref=src, dst_ref=dst, send_sem=send_sem, recv_sem=recv_sem,
            device_id=peer, device_id_type=MESH,
        )
        copy.start()

    def arrived(ref, send_sem, recv_sem):
        copy = pltpu.make_async_remote_copy(
            src_ref=ref, dst_ref=ref, send_sem=send_sem, recv_sem=recv_sem,
            device_id=y_peers[0], device_id_type=MESH,
        )
        copy.wait_recv()
        sends.append(copy)

    split = starts[-1] // TILE
    batches = (pl.ds(0, split), pl.ds(split, TILES - split))

    def send_stats(b):
        for k, peer in zip(y_index, y_peers):
            remote(
                ysend.at[k, batches[b]], yrecv.at[y, batches[b]], y_send.at[b], y_recv.at[b], peer
            )

    def got_stats(b):
        yrecv[y, batches[b]] = ysend[y, batches[b]]
        size = TILES - split if b else split
        whole = yrecv.at[pl.ds(0, NY - 1), pl.ds(0, size)]
        arrived(whole, y_send.at[b], y_recv.at[b])

    w_copy.wait()
    dot(0)
    for copy in small_copies:
        copy.wait()
    count = jnp.zeros((1, LANE), jnp.float32)
    for t in range(TILES):
        yid[y, t] = jnp.full((1, LANE), event[t].astype(jnp.float32))
        count += jnp.where(lane == event[t], live[t].astype(jnp.float32), 0.0)
    yid[y, TILES] = count
    for g in range(1, len(SIZES)):
        dot(g)
        stats(g - 1)
    pl.semaphore_wait(barrier, len(near))
    for peer in y_peers:
        remote(yid.at[y], yid.at[y], id_send, id_recv, peer)
    send_stats(0)
    for d in (HOP, NZ - HOP):
        pl.semaphore_signal(known, inc=1, device_id=z_peers[d - 1], device_id_type=MESH)
    stats(len(SIZES) - 1)
    send_stats(1)

    arrived(yid.at[pl.ds(0, NY - 1)], id_send, id_recv)
    count = yid[0, TILES]
    for s in range(1, NY):
        count += yid[s, TILES]
    crecv[z] = count
    index = lax.broadcasted_iota(jnp.int32, (EVENTS, LANE), 0).astype(jnp.float32)

    def chosen(s, t):
        member = jnp.broadcast_to(yid[s, t], (EVENTS, LANE)) == index
        return jnp.where(member, yrecv[s, t, 0:1, :], BIG)

    def merged(order, top, first, second):
        high = top
        for entry in order:
            high = jnp.maximum(high, chosen(*entry))
        keep = jnp.exp2((top - high) * LOG2E)
        first, second = first * keep, second * (keep * keep)
        for s, t in order:
            w = jnp.exp2((chosen(s, t) - high) * LOG2E)
            first += w
            second += w * w * yrecv[s, t, 1:2, :]
        return high, first, second

    zero = jnp.zeros((EVENTS, LANE), jnp.float32)
    got_stats(0)
    order = [(s, t) for t in range(split) for s in range(NY)]
    held[0], held[1], held[2] = merged(order, zero + BIG, zero, zero)
    got_stats(1)
    order = [(s, t) for t in range(split, TILES) for s in range(NY)]
    top, first, second = merged(order, held[0], held[1], held[2])
    lse, ratio = top + jnp.log(first), second / (first * first)
    for k in range(NZ):
        zsend[k, 0] = lse[k * OWN : (k + 1) * OWN, :]
        zsend[k, 1] = ratio[k * OWN : (k + 1) * OWN, :]

    pl.semaphore_wait(known, 2)
    for peer in z_peers:
        remote(crecv.at[z], crecv.at[z], c_send, c_recv, peer)
    for k, peer in zip(z_index, z_peers):
        remote(zsend.at[k], zrecv.at[z], z_send, z_recv, peer)
    zrecv[z] = zsend[z]

    arrived(crecv.at[pl.ds(0, NZ - 1)], c_send, c_recv)
    count = crecv[0]
    for k in range(1, NZ):
        count += crecv[k]
    row = lax.broadcasted_iota(jnp.int32, (OWN, LANE), 0)
    col = lax.broadcasted_iota(jnp.int32, (OWN, LANE), 1)
    count = jnp.where(col == row + z * OWN, jnp.broadcast_to(count, (OWN, LANE)), 0.0)
    count = jnp.broadcast_to(jnp.sum(count, axis=1, keepdims=True), (OWN, LANE))
    shift = offset_buf[pl.ds(y, 1), :] - jnp.log(count)
    arrived(zrecv.at[pl.ds(0, NZ - 1)], z_send, z_recv)
    top = zrecv[0, 0]
    for k in range(1, NZ):
        top = jnp.maximum(top, zrecv[k, 0])
    first = jnp.zeros((OWN, LANE), jnp.float32)
    second = jnp.zeros((OWN, LANE), jnp.float32)
    for k in range(NZ):
        w = jnp.exp2((zrecv[k, 0] - top) * LOG2E)
        first += w
        second += w * w * zrecv[k, 1]
    evidence = top + jnp.log(first) + shift
    lbuf[z] = jnp.sum(evidence, axis=0, keepdims=True)
    for peer in z_peers:
        remote(lbuf.at[z], lbuf.at[z], l_send, l_recv, peer)
    ess = first * first / (second * count)
    for i in range(NY):
        osend[i, 0:1, :] = evidence[i : i + 1, :]
        osend[i, 1:2, :] = ess[i : i + 1, :]
    for k, peer in zip(y_index, y_peers):
        remote(osend.at[k], orecv.at[y], o_send, o_recv, peer)
    orecv[y] = osend[y]

    arrived(lbuf.at[pl.ds(0, NZ - 1)], l_send, l_recv)
    loglik = lbuf[0]
    for k in range(1, NZ):
        loglik += lbuf[k]
    vbuf[gi * NJ + y] = loglik * (1.0 / EVENTS)
    for peer in v_peers:
        remote(vbuf.at[gi * NJ + y], vbuf.at[gi * NJ + y], v_send, v_recv, peer)
    arrived(orecv.at[pl.ds(0, NY - 1)], o_send, o_recv)
    for j in range(NJ):
        evidence_out[j : j + 1, :] = orecv[j, 0:1, :]
        ess_out[j : j + 1, :] = orecv[j, 1:2, :]
    arrived(vbuf.at[pl.ds(0, NG * NJ - 1)], v_send, v_recv)
    best = vbuf[0]
    for k in range(1, NG * NJ):
        best = jnp.maximum(best, vbuf[k])
    best = jnp.max(best)
    mass = jnp.zeros((1, LANE), jnp.float32)
    for k in range(NG * NJ):
        mass += jnp.exp2((vbuf[k] - best) * LOG2E)
    norm = best + jnp.log(jnp.full((1, LANE), jnp.sum(mass)))
    for j in range(NJ):
        posterior_out[j : j + 1, :] = vbuf[gi * NJ + j] - norm

    for copy in sends:
        copy.wait_send()


def finish(evidence, ess, posterior, evidence_out, ess_out, posterior_out, sem):
    pairs = ((evidence, evidence_out), (ess, ess_out), (posterior, posterior_out))
    copies = [pltpu.make_async_copy(a, b, sem.at[k]) for k, (a, b) in enumerate(pairs)]
    for copy in copies:
        copy.start()
    for copy in copies:
        copy.wait()


def body(summary, weight, offset, prior, event, live):
    rows, bins = summary.shape
    cols = weight.shape[1]
    dma, vmem, smem = pltpu.SemaphoreType.DMA, pltpu.VMEM, pltpu.SMEM
    f32 = jnp.float32
    hbm = pl.BlockSpec(memory_space=pltpu.HBM)
    local = pl.BlockSpec(memory_space=pltpu.VMEM)
    kept = vmem((NJ, LANE), f32)
    outs = pl.pallas_call(
        kernel,
        name="reweight",
        out_shape=(kept, kept, kept),
        in_specs=[hbm] * 6,
        out_specs=(local,) * 3,
        scratch_shapes=[
            vmem((rows, bins), jnp.bfloat16),
            vmem((bins, cols), jnp.bfloat16),
            vmem((2, max(SIZES), cols), f32),
            vmem((TILES, LANE), f32),
            vmem((NJ, LANE), f32),
            smem((TILES,), jnp.int32),
            smem((TILES,), jnp.int32),
            vmem((NY, TILES + 1, 1, LANE), f32),
            vmem((NJ, TILES, 2, LANE), f32),
            vmem((NY, TILES, 2, LANE), f32),
            vmem((3, EVENTS, LANE), f32),
            vmem((NZ, 2, OWN, LANE), f32),
            vmem((NZ, 2, OWN, LANE), f32),
            vmem((NZ, 1, LANE), f32),
            vmem((NZ, 1, LANE), f32),
            vmem((NY, 2, LANE), f32),
            vmem((NY, 2, LANE), f32),
            vmem((NG * NJ, 1, LANE), f32),
            dma((5,)),
            dma((len(SIZES),)),
            dma, dma,
            dma((2,)),
            dma((2,)),
            dma, dma, dma, dma, dma, dma, dma, dma, dma, dma,
            pltpu.SemaphoreType.REGULAR,
        ],
        compiler_params=pltpu.CompilerParams(
            collective_id=0, has_side_effects=True, vmem_limit_bytes=32 * 1024 * 1024
        ),
        cost_estimate=pl.CostEstimate(
            flops=2 * rows * bins * cols, bytes_accessed=2 * rows * bins, transcendentals=rows * cols
        ),
    )(*(
        pltpu.with_memory_space_constraint(a, pltpu.HBM)
        for a in (summary, weight, prior.reshape(TILES, LANE), offset.reshape(NJ, LANE), event, live)
    ))
    small = jax.ShapeDtypeStruct((NJ, LANE), f32)
    evidence, ess, posterior = pl.pallas_call(
        finish,
        name="finish",
        out_shape=(small, small, small),
        in_specs=[local] * 3,
        out_specs=(hbm,) * 3,
        scratch_shapes=[dma((3,))],
        compiler_params=pltpu.CompilerParams(vmem_limit_bytes=1024 * 1024),
    )(*outs)
    return evidence.reshape(1, cols), ess.reshape(1, cols), posterior.reshape(cols)


def solution(mesh):
    in_specs = (P("samp", None), P(None, "grid"), P("grid"), P("samp"), P("samp"), P("samp"))
    out_specs = (P("samp", "grid"), P("samp", "grid"), P("grid"))
    return jax.shard_map(body, mesh=mesh, in_specs=in_specs, out_specs=out_specs, check_vma=False)
```

time: 55 us -> 41.8 us (0.76)
  local copies, waits for them, and re-layouts: 7.83 us -> 0 us
  Pallas kernels: 46.2 us -> 41 us
    unnamed x15 -> x0, local copies, waits for them, and re-layouts: 7.83 us -> none
    pallas_call x1 -> x2, Pallas kernels: 46.2 us -> 41 us  [the longest x1 40.4 us: body(): pl.pallas_call(kernel, name='reweight', out_shape=(kept, kept, kept), in_...]
where the time goes in v3:
time: 41.8 us; the launch traced here: 41.6 us
  Pallas kernels  41 us (98%)
  between operations  0.64 us (2%)
    pallas_call x1, Pallas kernels, body(): pl.pallas_call(kernel, name='reweight', out_shape=(kept, kept, kept), in_...  40.4 us

profile of v3, /device:TPU:1, one launch (start us, length us, event | category | flops | bytes accessed | tf_op | source)
XLA Modules:
  0.0 41.6 jit_solution(7397333381705275226)
XLA Ops:
  0.6 40.4 %reweight.1 = (f32[4,128]{1,0:T(4,128)S(1)}, f32[4,128]{1,0:T(4,128)S(1)}, f32[4,128]{1,0:T(4,128)S(1)}) custom-call(bf16[2048,1024]{1,0:T(8,128)(2,1)} %summary.1, bf16[1024,512]{1,0:T(8,128)(2,1)} %weight.1, f32[16,128]{1,0:T(8,128)} %bitcast.5, f32[4,128]{1,0:T(4,128)} %bitcast.6, s32[16]{0:T(128)} %event_in.1, s32[16]{0:T(128)} %live_in.1), custom_call_target="tpu_custom_call" | custom-call | flops 2147483648 | bytes 4194304 | tf_op jit(solution)/shard_map/reweight/pallas_call | solution.py:267
  41.0 0.6 %finish.1 = (f32[4,128]{1,0:T(4,128)}, f32[4,128]{1,0:T(4,128)}, f32[4,128]{1,0:T(4,128)}) custom-call(f32[4,128]{1,0:T(4,128)S(1)} %get-tuple-element.9.evidence, f32[4,128]{1,0:T(4,128)S(1)} %get-tuple-element.10.ess, f32[4,128]{1,0:T(4,128)S(1)} %get-tuple-element.11.posterior), custom_call_target="tpu_custom_call" | custom-call | tf_op jit(solution)/shard_map/finish/pallas_call | solution.py:311

commit v4 on v3

--- a/solution.py
+++ b/solution.py
@@ -14,7 +14,8 @@
 TILES = 16
 OWN = EVENTS // NZ
 SIZES = (256, 512, 512, 512, 256)
-AHEAD = 2
+WAITS = 3
+ROOT = 0
 HOP = 4
 BIG = -1e30
 LOG2E = 1.4426950408889634
@@ -25,9 +26,9 @@
     summary, weight, prior, offset, event_in, live_in,
     evidence_out, ess_out, posterior_out,
     x_buf, w_buf, scores, prior_buf, offset_buf, event, live,
-    yid, ysend, yrecv, held, zsend, zrecv, crecv, lbuf, osend, orecv, vbuf,
+    yid, ysend, yrecv, held, lse, lse_all, zsend, zrecv, crecv, osend, orecv, vbuf, pbuf,
     in_sem, x_sem, id_send, id_recv, y_send, y_recv, c_send, c_recv, z_send, z_recv,
-    l_send, l_recv, o_send, o_recv, v_send, v_recv, known,
+    l_send, l_recv, o_send, o_recv, v_send, v_recv, p_send, p_recv, known,
 ):
     gi, si = lax.axis_index("grid"), lax.axis_index("samp")
     x, c = gi // NC, lax.rem(gi, NC)
@@ -44,10 +45,7 @@
     w_copy, *small_copies = [
         pltpu.make_async_copy(a, b, in_sem.at[k]) for k, (a, b) in enumerate(pairs)
     ]
-    w_copy.start()
-    for copy in x_copies[:AHEAD]:
-        copy.start()
-    for copy in small_copies:
+    for copy in (*small_copies, w_copy, *x_copies):
         copy.start()
 
     y_index = [lax.rem(y + d, NY) for d in range(1, NY)]
@@ -72,9 +70,9 @@
     lane = lax.broadcasted_iota(jnp.int32, (1, LANE), 1)
 
     def dot(g):
-        x_copies[g].wait()
-        if g + AHEAD < len(SIZES):
-            x_copies[g + AHEAD].start()
+        if g < WAITS:
+            for copy in x_copies[g:] if g == WAITS - 1 else x_copies[g : g + 1]:
+                copy.wait()
         scores[g % 2, : SIZES[g], :] = jnp.dot(
             x_buf[starts[g] : starts[g] + SIZES[g], :], w_buf[...],
             preferred_element_type=jnp.float32,
@@ -94,8 +92,6 @@
                 ysend[j, t, 0:1, :] = top + jnp.log(first)
                 ysend[j, t, 1:2, :] = second / (first * first)
 
-    sends = []
-
     def remote(src, dst, send_sem, recv_sem, peer):
         copy = pltpu.make_async_remote_copy(
             src_ref=src, dst_ref=dst, send_sem=send_sem, recv_sem=recv_sem,
@@ -103,13 +99,16 @@
         )
         copy.start()
 
-    def arrived(ref, send_sem, recv_sem):
-        copy = pltpu.make_async_remote_copy(
+    def moved(ref, send_sem, recv_sem):
+        return pltpu.make_async_remote_copy(
             src_ref=ref, dst_ref=ref, send_sem=send_sem, recv_sem=recv_sem,
             device_id=y_peers[0], device_id_type=MESH,
         )
-        copy.wait_recv()
-        sends.append(copy)
+
+    id_moved = moved(yid.at[pl.ds(0, NY - 1)], id_send, id_recv)
+    c_moved = moved(crecv.at[pl.ds(0, NZ - 1)], c_send, c_recv)
+    z_moved = moved(zrecv.at[pl.ds(0, NZ - 1)], z_send, z_recv)
+    o_moved = moved(orecv.at[pl.ds(0, NY - 1)], o_send, o_recv)
 
     split = starts[-1] // TILE
     batches = (pl.ds(0, split), pl.ds(split, TILES - split))
@@ -120,14 +119,14 @@
                 ysend.at[k, batches[b]], yrecv.at[y, batches[b]], y_send.at[b], y_recv.at[b], peer
             )
 
+    def stats_moved(b):
+        size = TILES - split if b else split
+        return moved(yrecv.at[pl.ds(0, NY - 1), pl.ds(0, size)], y_send.at[b], y_recv.at[b])
+
     def got_stats(b):
         yrecv[y, batches[b]] = ysend[y, batches[b]]
-        size = TILES - split if b else split
-        whole = yrecv.at[pl.ds(0, NY - 1), pl.ds(0, size)]
-        arrived(whole, y_send.at[b], y_recv.at[b])
-
-    w_copy.wait()
-    dot(0)
+        stats_moved(b).wait_recv()
+
     for copy in small_copies:
         copy.wait()
     count = jnp.zeros((1, LANE), jnp.float32)
@@ -135,6 +134,8 @@
         yid[y, t] = jnp.full((1, LANE), event[t].astype(jnp.float32))
         count += jnp.where(lane == event[t], live[t].astype(jnp.float32), 0.0)
     yid[y, TILES] = count
+    w_copy.wait()
+    dot(0)
     for g in range(1, len(SIZES)):
         dot(g)
         stats(g - 1)
@@ -147,7 +148,7 @@
     stats(len(SIZES) - 1)
     send_stats(1)
 
-    arrived(yid.at[pl.ds(0, NY - 1)], id_send, id_recv)
+    id_moved.wait_recv()
     count = yid[0, TILES]
     for s in range(1, NY):
         count += yid[s, TILES]
@@ -174,31 +175,55 @@
     got_stats(0)
     order = [(s, t) for t in range(split) for s in range(NY)]
     held[0], held[1], held[2] = merged(order, zero + BIG, zero, zero)
+    pl.semaphore_wait(known, 2)
+    for peer in z_peers:
+        remote(crecv.at[z], crecv.at[z], c_send, c_recv, peer)
     got_stats(1)
     order = [(s, t) for t in range(split, TILES) for s in range(NY)]
     top, first, second = merged(order, held[0], held[1], held[2])
-    lse, ratio = top + jnp.log(first), second / (first * first)
+    lse[...] = top + jnp.log(first)
+
+    @pl.when(z != ROOT)
+    def _():
+        remote(lse, lse_all.at[z], l_send, l_recv, (gi, ROOT * NY + y))
+
+    ratio = second / (first * first)
     for k in range(NZ):
         zsend[k, 0] = lse[k * OWN : (k + 1) * OWN, :]
         zsend[k, 1] = ratio[k * OWN : (k + 1) * OWN, :]
-
-    pl.semaphore_wait(known, 2)
-    for peer in z_peers:
-        remote(crecv.at[z], crecv.at[z], c_send, c_recv, peer)
     for k, peer in zip(z_index, z_peers):
         remote(zsend.at[k], zrecv.at[z], z_send, z_recv, peer)
     zrecv[z] = zsend[z]
 
-    arrived(crecv.at[pl.ds(0, NZ - 1)], c_send, c_recv)
+    c_moved.wait_recv()
     count = crecv[0]
     for k in range(1, NZ):
         count += crecv[k]
+    shift = offset_buf[pl.ds(y, 1), :]
+    v_moved = moved(vbuf.at[pl.ds(0, NG * NJ - 1)], v_send, v_recv)
+
+    @pl.when(z == ROOT)
+    def _():
+        logs = jnp.sum(jnp.where(lane < EVENTS, jnp.log(jnp.maximum(count, 1.0)), 0.0))
+        lse_all[ROOT] = lse[...]
+        moved(lse_all.at[pl.ds(0, NZ - 1)], l_send, l_recv).wait_recv()
+        top = lse_all[0]
+        for k in range(1, NZ):
+            top = jnp.maximum(top, lse_all[k])
+        first = jnp.zeros((EVENTS, LANE), jnp.float32)
+        for k in range(NZ):
+            first += jnp.exp2((lse_all[k] - top) * LOG2E)
+        line = jnp.sum(top + jnp.log(first), axis=0, keepdims=True)
+        vbuf[gi * NJ + y] = (line - logs) * (1.0 / EVENTS) + shift
+        for peer in v_peers:
+            remote(vbuf.at[gi * NJ + y], vbuf.at[gi * NJ + y], v_send, v_recv, peer)
+
     row = lax.broadcasted_iota(jnp.int32, (OWN, LANE), 0)
     col = lax.broadcasted_iota(jnp.int32, (OWN, LANE), 1)
     count = jnp.where(col == row + z * OWN, jnp.broadcast_to(count, (OWN, LANE)), 0.0)
     count = jnp.broadcast_to(jnp.sum(count, axis=1, keepdims=True), (OWN, LANE))
-    shift = offset_buf[pl.ds(y, 1), :] - jnp.log(count)
-    arrived(zrecv.at[pl.ds(0, NZ - 1)], z_send, z_recv)
+    shift = shift - jnp.log(count)
+    z_moved.wait_recv()
     top = zrecv[0, 0]
     for k in range(1, NZ):
         top = jnp.maximum(top, zrecv[k, 0])
@@ -209,9 +234,6 @@
         first += w
         second += w * w * zrecv[k, 1]
     evidence = top + jnp.log(first) + shift
-    lbuf[z] = jnp.sum(evidence, axis=0, keepdims=True)
-    for peer in z_peers:
-        remote(lbuf.at[z], lbuf.at[z], l_send, l_recv, peer)
     ess = first * first / (second * count)
     for i in range(NY):
         osend[i, 0:1, :] = evidence[i : i + 1, :]
@@ -220,31 +242,42 @@
         remote(osend.at[k], orecv.at[y], o_send, o_recv, peer)
     orecv[y] = osend[y]
 
-    arrived(lbuf.at[pl.ds(0, NZ - 1)], l_send, l_recv)
-    loglik = lbuf[0]
-    for k in range(1, NZ):
-        loglik += lbuf[k]
-    vbuf[gi * NJ + y] = loglik * (1.0 / EVENTS)
-    for peer in v_peers:
-        remote(vbuf.at[gi * NJ + y], vbuf.at[gi * NJ + y], v_send, v_recv, peer)
-    arrived(orecv.at[pl.ds(0, NY - 1)], o_send, o_recv)
+    @pl.when(z == ROOT)
+    def _():
+        v_moved.wait_recv()
+        best = vbuf[0]
+        for k in range(1, NG * NJ):
+            best = jnp.maximum(best, vbuf[k])
+        best = jnp.max(best)
+        mass = jnp.zeros((1, LANE), jnp.float32)
+        for k in range(NG * NJ):
+            mass += jnp.exp2((vbuf[k] - best) * LOG2E)
+        norm = best + jnp.log(jnp.full((1, LANE), jnp.sum(mass)))
+        for j in range(NJ):
+            pbuf[j : j + 1, :] = vbuf[gi * NJ + j] - norm
+        for peer in z_peers:
+            remote(pbuf, pbuf, p_send, p_recv, peer)
+
+    o_moved.wait_recv()
     for j in range(NJ):
         evidence_out[j : j + 1, :] = orecv[j, 0:1, :]
         ess_out[j : j + 1, :] = orecv[j, 1:2, :]
-    arrived(vbuf.at[pl.ds(0, NG * NJ - 1)], v_send, v_recv)
-    best = vbuf[0]
-    for k in range(1, NG * NJ):
-        best = jnp.maximum(best, vbuf[k])
-    best = jnp.max(best)
-    mass = jnp.zeros((1, LANE), jnp.float32)
-    for k in range(NG * NJ):
-        mass += jnp.exp2((vbuf[k] - best) * LOG2E)
-    norm = best + jnp.log(jnp.full((1, LANE), jnp.sum(mass)))
-    for j in range(NJ):
-        posterior_out[j : j + 1, :] = vbuf[gi * NJ + j] - norm
-
-    for copy in sends:
+
+    for copy in (id_moved, c_moved, z_moved, o_moved, stats_moved(0), stats_moved(1)):
         copy.wait_send()
+
+    @pl.when(z != ROOT)
+    def _():
+        moved(lse, l_send, l_recv).wait_send()
+        moved(pbuf, p_send, p_recv).wait_recv()
+
+    @pl.when(z == ROOT)
+    def _():
+        v_moved.wait_send()
+        for _ in range(NZ - 1):
+            moved(pbuf, p_send, p_recv).wait_send()
+
+    posterior_out[...] = pbuf[...]
 
 
 def finish(evidence, ess, posterior, evidence_out, ess_out, posterior_out, sem):
@@ -282,19 +315,21 @@
             vmem((NJ, TILES, 2, LANE), f32),
             vmem((NY, TILES, 2, LANE), f32),
             vmem((3, EVENTS, LANE), f32),
+            vmem((EVENTS, LANE), f32),
+            vmem((NZ, EVENTS, LANE), f32),
             vmem((NZ, 2, OWN, LANE), f32),
             vmem((NZ, 2, OWN, LANE), f32),
-            vmem((NZ, 1, LANE), f32),
             vmem((NZ, 1, LANE), f32),
             vmem((NY, 2, LANE), f32),
             vmem((NY, 2, LANE), f32),
             vmem((NG * NJ, 1, LANE), f32),
+            vmem((NJ, LANE), f32),
             dma((5,)),
             dma((len(SIZES),)),
             dma, dma,
             dma((2,)),
             dma((2,)),
-            dma, dma, dma, dma, dma, dma, dma, dma, dma, dma,
+            dma, dma, dma, dma, dma, dma, dma, dma, dma, dma, dma, dma,
             pltpu.SemaphoreType.REGULAR,
         ],
         compiler_params=pltpu.CompilerParams(

time: 41.8 us -> 39.6 us (0.947)
  Pallas kernels: 41 us -> 38.8 us
    pallas_call x1, Pallas kernels: 40.4 us -> 38.2 us  [body(): pl.pallas_call(kernel, name='reweight', out_shape=(kept, kept, kept), in_...]
where the time goes in v4:
time: 39.6 us; the launch traced here: 39.4 us
  Pallas kernels  38.8 us (98%)
  between operations  0.64 us (2%)
    pallas_call x1, Pallas kernels, body(): pl.pallas_call(kernel, name='reweight', out_shape=(kept, kept, kept), in_...  38.2 us

profile of v4, /device:TPU:1, one launch (start us, length us, event | category | flops | bytes accessed | tf_op | source)
XLA Modules:
  0.0 39.4 jit_solution(43618374511252533)
XLA Ops:
  0.6 38.2 %reweight.1 = (f32[4,128]{1,0:T(4,128)S(1)}, f32[4,128]{1,0:T(4,128)S(1)}, f32[4,128]{1,0:T(4,128)S(1)}) custom-call(bf16[2048,1024]{1,0:T(8,128)(2,1)} %summary.1, bf16[1024,512]{1,0:T(8,128)(2,1)} %weight.1, f32[16,128]{1,0:T(8,128)} %bitcast.5, f32[4,128]{1,0:T(4,128)} %bitcast.6, s32[16]{0:T(128)} %event_in.1, s32[16]{0:T(128)} %live_in.1), custom_call_target="tpu_custom_call" | custom-call | flops 2147483648 | bytes 4194304 | tf_op jit(solution)/shard_map/reweight/pallas_call | solution.py:300
  38.8 0.6 %finish.1 = (f32[4,128]{1,0:T(4,128)}, f32[4,128]{1,0:T(4,128)}, f32[4,128]{1,0:T(4,128)}) custom-call(f32[4,128]{1,0:T(4,128)S(1)} %get-tuple-element.9.evidence, f32[4,128]{1,0:T(4,128)S(1)} %get-tuple-element.10.ess, f32[4,128]{1,0:T(4,128)S(1)} %get-tuple-element.11.posterior), custom_call_target="tpu_custom_call" | custom-call | tf_op jit(solution)/shard_map/finish/pallas_call | solution.py:346

commit v5 on v4

--- a/solution.py
+++ b/solution.py
@@ -12,7 +12,6 @@
 LANE = 128
 NJ = 4
 TILES = 16
-OWN = EVENTS // NZ
 SIZES = (256, 512, 512, 512, 256)
 WAITS = 3
 ROOT = 0
@@ -26,9 +25,9 @@
     summary, weight, prior, offset, event_in, live_in,
     evidence_out, ess_out, posterior_out,
     x_buf, w_buf, scores, prior_buf, offset_buf, event, live,
-    yid, ysend, yrecv, held, lse, lse_all, zsend, zrecv, crecv, osend, orecv, vbuf, pbuf,
+    yid, ysend, yrecv, held, lse, lse_all, zsend, zrecv, crecv, vbuf, pbuf,
     in_sem, x_sem, id_send, id_recv, y_send, y_recv, c_send, c_recv, z_send, z_recv,
-    l_send, l_recv, o_send, o_recv, v_send, v_recv, p_send, p_recv, known,
+    l_send, l_recv, v_send, v_recv, p_send, p_recv, known,
 ):
     gi, si = lax.axis_index("grid"), lax.axis_index("samp")
     x, c = gi // NC, lax.rem(gi, NC)
@@ -107,8 +106,7 @@
 
     id_moved = moved(yid.at[pl.ds(0, NY - 1)], id_send, id_recv)
     c_moved = moved(crecv.at[pl.ds(0, NZ - 1)], c_send, c_recv)
-    z_moved = moved(zrecv.at[pl.ds(0, NZ - 1)], z_send, z_recv)
-    o_moved = moved(orecv.at[pl.ds(0, NY - 1)], o_send, o_recv)
+    z_moved = moved(zrecv.at[pl.ds(0, EVENTS - 1)], z_send, z_recv)
 
     split = starts[-1] // TILE
     batches = (pl.ds(0, split), pl.ds(split, TILES - split))
@@ -144,7 +142,7 @@
         remote(yid.at[y], yid.at[y], id_send, id_recv, peer)
     send_stats(0)
     for d in (HOP, NZ - HOP):
-        pl.semaphore_signal(known, inc=1, device_id=z_peers[d - 1], device_id_type=MESH)
+        pl.semaphore_signal(known.at[0], inc=1, device_id=z_peers[d - 1], device_id_type=MESH)
     stats(len(SIZES) - 1)
     send_stats(1)
 
@@ -175,7 +173,9 @@
     got_stats(0)
     order = [(s, t) for t in range(split) for s in range(NY)]
     held[0], held[1], held[2] = merged(order, zero + BIG, zero, zero)
-    pl.semaphore_wait(known, 2)
+    pl.semaphore_wait(known.at[0], 2)
+    for peer in y_peers:
+        pl.semaphore_signal(known.at[1], inc=1, device_id=peer, device_id_type=MESH)
     for peer in z_peers:
         remote(crecv.at[z], crecv.at[z], c_send, c_recv, peer)
     got_stats(1)
@@ -188,18 +188,21 @@
         remote(lse, lse_all.at[z], l_send, l_recv, (gi, ROOT * NY + y))
 
     ratio = second / (first * first)
-    for k in range(NZ):
-        zsend[k, 0] = lse[k * OWN : (k + 1) * OWN, :]
-        zsend[k, 1] = ratio[k * OWN : (k + 1) * OWN, :]
-    for k, peer in zip(z_index, z_peers):
-        remote(zsend.at[k], zrecv.at[z], z_send, z_recv, peer)
-    zrecv[z] = zsend[z]
-
+    for k in range(EVENTS):
+        zsend[k, 0:1, :] = lse[k : k + 1, :]
+        zsend[k, 1:2, :] = ratio[k : k + 1, :]
+    zrecv[si] = zsend[si]
+    pl.semaphore_wait(known.at[1], NY - 1)
     c_moved.wait_recv()
+    for dz in sorted(range(NZ), key=lambda d: abs(d - NZ // 2)):
+        for dy in range(NY):
+            if dz or dy:
+                k = lax.rem(z + dz, NZ) * NY + lax.rem(y + dy, NY)
+                remote(zsend.at[k], zrecv.at[si], z_send, z_recv, (gi, k))
+
     count = crecv[0]
     for k in range(1, NZ):
         count += crecv[k]
-    shift = offset_buf[pl.ds(y, 1), :]
     v_moved = moved(vbuf.at[pl.ds(0, NG * NJ - 1)], v_send, v_recv)
 
     @pl.when(z == ROOT)
@@ -214,33 +217,25 @@
         for k in range(NZ):
             first += jnp.exp2((lse_all[k] - top) * LOG2E)
         line = jnp.sum(top + jnp.log(first), axis=0, keepdims=True)
-        vbuf[gi * NJ + y] = (line - logs) * (1.0 / EVENTS) + shift
+        vbuf[gi * NJ + y] = (line - logs) * (1.0 / EVENTS) + offset_buf[pl.ds(y, 1), :]
         for peer in v_peers:
             remote(vbuf.at[gi * NJ + y], vbuf.at[gi * NJ + y], v_send, v_recv, peer)
 
-    row = lax.broadcasted_iota(jnp.int32, (OWN, LANE), 0)
-    col = lax.broadcasted_iota(jnp.int32, (OWN, LANE), 1)
-    count = jnp.where(col == row + z * OWN, jnp.broadcast_to(count, (OWN, LANE)), 0.0)
-    count = jnp.broadcast_to(jnp.sum(count, axis=1, keepdims=True), (OWN, LANE))
-    shift = shift - jnp.log(count)
+    count = jnp.full((1, LANE), jnp.sum(jnp.where(lane == si, count, 0.0)))
     z_moved.wait_recv()
-    top = zrecv[0, 0]
-    for k in range(1, NZ):
-        top = jnp.maximum(top, zrecv[k, 0])
-    first = jnp.zeros((OWN, LANE), jnp.float32)
-    second = jnp.zeros((OWN, LANE), jnp.float32)
-    for k in range(NZ):
-        w = jnp.exp2((zrecv[k, 0] - top) * LOG2E)
-        first += w
-        second += w * w * zrecv[k, 1]
-    evidence = top + jnp.log(first) + shift
-    ess = first * first / (second * count)
-    for i in range(NY):
-        osend[i, 0:1, :] = evidence[i : i + 1, :]
-        osend[i, 1:2, :] = ess[i : i + 1, :]
-    for k, peer in zip(y_index, y_peers):
-        remote(osend.at[k], orecv.at[y], o_send, o_recv, peer)
-    orecv[y] = osend[y]
+    for j in range(NJ):
+        top = zrecv[j, 0:1, :]
+        for k in range(1, NZ):
+            top = jnp.maximum(top, zrecv[k * NY + j, 0:1, :])
+        first = jnp.zeros((1, LANE), jnp.float32)
+        second = jnp.zeros((1, LANE), jnp.float32)
+        for k in range(NZ):
+            w = jnp.exp2((zrecv[k * NY + j, 0:1, :] - top) * LOG2E)
+            first += w
+            second += w * w * zrecv[k * NY + j, 1:2, :]
+        shift = offset_buf[j : j + 1, :] - jnp.log(count)
+        evidence_out[j : j + 1, :] = top + jnp.log(first) + shift
+        ess_out[j : j + 1, :] = first * first / (second * count)
 
     @pl.when(z == ROOT)
     def _():
@@ -258,12 +253,7 @@
         for peer in z_peers:
             remote(pbuf, pbuf, p_send, p_recv, peer)
 
-    o_moved.wait_recv()
-    for j in range(NJ):
-        evidence_out[j : j + 1, :] = orecv[j, 0:1, :]
-        ess_out[j : j + 1, :] = orecv[j, 1:2, :]
-
-    for copy in (id_moved, c_moved, z_moved, o_moved, stats_moved(0), stats_moved(1)):
+    for copy in (id_moved, c_moved, z_moved, stats_moved(0), stats_moved(1)):
         copy.wait_send()
 
     @pl.when(z != ROOT)
@@ -317,11 +307,9 @@
             vmem((3, EVENTS, LANE), f32),
             vmem((EVENTS, LANE), f32),
             vmem((NZ, EVENTS, LANE), f32),
-            vmem((NZ, 2, OWN, LANE), f32),
-            vmem((NZ, 2, OWN, LANE), f32),
+            vmem((EVENTS, 2, LANE), f32),
+            vmem((EVENTS, 2, LANE), f32),
             vmem((NZ, 1, LANE), f32),
-            vmem((NY, 2, LANE), f32),
-            vmem((NY, 2, LANE), f32),
             vmem((NG * NJ, 1, LANE), f32),
             vmem((NJ, LANE), f32),
             dma((5,)),
@@ -329,8 +317,8 @@
             dma, dma,
             dma((2,)),
             dma((2,)),
-            dma, dma, dma, dma, dma, dma, dma, dma, dma, dma, dma, dma,
-            pltpu.SemaphoreType.REGULAR,
+            dma, dma, dma, dma, dma, dma, dma, dma, dma, dma,
+            pltpu.SemaphoreType.REGULAR((2,)),
         ],
         compiler_params=pltpu.CompilerParams(
             collective_id=0, has_side_effects=True, vmem_limit_bytes=32 * 1024 * 1024

time: 39.6 us -> 37.6 us (0.949)
  Pallas kernels: 38.8 us -> 36.8 us
    pallas_call x1, Pallas kernels: 38.2 us -> 36.2 us  [body(): pl.pallas_call(kernel, name='reweight', out_shape=(kept, kept, kept), in_...]
where the time goes in v5:
time: 37.6 us; the launch traced here: 37.4 us
  Pallas kernels  36.8 us (98%)
  between operations  0.64 us (2%)
    pallas_call x1, Pallas kernels, body(): pl.pallas_call(kernel, name='reweight', out_shape=(kept, kept, kept), in_...  36.2 us

profile of v5, /device:TPU:1, one launch (start us, length us, event | category | flops | bytes accessed | tf_op | source)
XLA Modules:
  0.0 37.4 jit_solution(6793744920813553484)
XLA Ops:
  0.6 36.2 %reweight.1 = (f32[4,128]{1,0:T(4,128)S(1)}, f32[4,128]{1,0:T(4,128)S(1)}, f32[4,128]{1,0:T(4,128)S(1)}) custom-call(bf16[2048,1024]{1,0:T(8,128)(2,1)} %summary.1, bf16[1024,512]{1,0:T(8,128)(2,1)} %weight.1, f32[16,128]{1,0:T(8,128)} %bitcast.5, f32[4,128]{1,0:T(4,128)} %bitcast.6, s32[16]{0:T(128)} %event_in.1, s32[16]{0:T(128)} %live_in.1), custom_call_target="tpu_custom_call" | custom-call | flops 2147483648 | bytes 4194304 | tf_op jit(solution)/shard_map/reweight/pallas_call | solution.py:290
  36.8 0.6 %finish.1 = (f32[4,128]{1,0:T(4,128)}, f32[4,128]{1,0:T(4,128)}, f32[4,128]{1,0:T(4,128)}) custom-call(f32[4,128]{1,0:T(4,128)S(1)} %get-tuple-element.9.evidence, f32[4,128]{1,0:T(4,128)S(1)} %get-tuple-element.10.ess, f32[4,128]{1,0:T(4,128)S(1)} %get-tuple-element.11.posterior), custom_call_target="tpu_custom_call" | custom-call | tf_op jit(solution)/shard_map/finish/pallas_call | solution.py:334

commit v6 on v5

--- a/solution.py
+++ b/solution.py
@@ -25,9 +25,9 @@
     summary, weight, prior, offset, event_in, live_in,
     evidence_out, ess_out, posterior_out,
     x_buf, w_buf, scores, prior_buf, offset_buf, event, live,
-    yid, ysend, yrecv, held, lse, lse_all, zsend, zrecv, crecv, vbuf, pbuf,
+    yid, ysend, yrecv, held, lse, lse_all, zsend, zrecv, crecv, vbuf,
     in_sem, x_sem, id_send, id_recv, y_send, y_recv, c_send, c_recv, z_send, z_recv,
-    l_send, l_recv, v_send, v_recv, p_send, p_recv, known,
+    l_send, l_recv, v_send, v_recv, r_send, r_recv, known,
 ):
     gi, si = lax.axis_index("grid"), lax.axis_index("samp")
     x, c = gi // NC, lax.rem(gi, NC)
@@ -52,12 +52,12 @@
     z_index = [lax.rem(z + d, NZ) for d in range(1, NZ)]
     z_peers = [(gi, k * NY + y) for k in z_index]
     grid_peers, v_peers = [], []
-    for dx in range(NX):
-        for dc in range(NC):
-            grid = lax.rem(x + dx, NX) * NC + lax.rem(c + dc, NC)
-            if dx or dc:
-                grid_peers.append((grid, si))
-            for dy in range(NY):
+    for dx in (2, 1, 3, 0):
+        for dy in (2, 1, 3, 0):
+            for dc in (1, 0):
+                grid = lax.rem(x + dx, NX) * NC + lax.rem(c + dc, NC)
+                if not dy and (dx or dc):
+                    grid_peers.append((grid, si))
                 if dx or dc or dy:
                     v_peers.append((grid, z * NY + lax.rem(y + dy, NY)))
 
@@ -203,7 +203,14 @@
     count = crecv[0]
     for k in range(1, NZ):
         count += crecv[k]
+    own = gi * NJ + y
     v_moved = moved(vbuf.at[pl.ds(0, NG * NJ - 1)], v_send, v_recv)
+    row_moved = moved(vbuf.at[0], r_send, r_recv)
+
+    def send_plane():
+        for peer in v_peers:
+            remote(vbuf.at[own], vbuf.at[own], v_send, v_recv, peer)
+
 
     @pl.when(z == ROOT)
     def _():
@@ -217,9 +224,15 @@
         for k in range(NZ):
             first += jnp.exp2((lse_all[k] - top) * LOG2E)
         line = jnp.sum(top + jnp.log(first), axis=0, keepdims=True)
-        vbuf[gi * NJ + y] = (line - logs) * (1.0 / EVENTS) + offset_buf[pl.ds(y, 1), :]
-        for peer in v_peers:
-            remote(vbuf.at[gi * NJ + y], vbuf.at[gi * NJ + y], v_send, v_recv, peer)
+        vbuf[own] = (line - logs) * (1.0 / EVENTS) + offset_buf[pl.ds(y, 1), :]
+        send_plane()
+        for d in sorted(range(1, NZ), key=lambda d: abs(d - NZ // 2)):
+            remote(vbuf.at[own], vbuf.at[own], r_send, r_recv, z_peers[d - 1])
+
+    @pl.when(z != ROOT)
+    def _():
+        row_moved.wait_recv()
+        send_plane()
 
     count = jnp.full((1, LANE), jnp.sum(jnp.where(lane == si, count, 0.0)))
     z_moved.wait_recv()
@@ -237,37 +250,28 @@
         evidence_out[j : j + 1, :] = top + jnp.log(first) + shift
         ess_out[j : j + 1, :] = first * first / (second * count)
 
+    v_moved.wait_recv()
+    best = vbuf[0]
+    for k in range(1, NG * NJ):
+        best = jnp.maximum(best, vbuf[k])
+    best = jnp.max(best)
+    mass = jnp.zeros((1, LANE), jnp.float32)
+    for k in range(NG * NJ):
+        mass += jnp.exp2((vbuf[k] - best) * LOG2E)
+    norm = best + jnp.log(jnp.full((1, LANE), jnp.sum(mass)))
+    for j in range(NJ):
+        posterior_out[j : j + 1, :] = vbuf[gi * NJ + j] - norm
+
+    for copy in (id_moved, c_moved, z_moved, v_moved, stats_moved(0), stats_moved(1)):
+        copy.wait_send()
+
+    @pl.when(z != ROOT)
+    def _():
+        moved(lse, l_send, l_recv).wait_send()
+
     @pl.when(z == ROOT)
     def _():
-        v_moved.wait_recv()
-        best = vbuf[0]
-        for k in range(1, NG * NJ):
-            best = jnp.maximum(best, vbuf[k])
-        best = jnp.max(best)
-        mass = jnp.zeros((1, LANE), jnp.float32)
-        for k in range(NG * NJ):
-            mass += jnp.exp2((vbuf[k] - best) * LOG2E)
-        norm = best + jnp.log(jnp.full((1, LANE), jnp.sum(mass)))
-        for j in range(NJ):
-            pbuf[j : j + 1, :] = vbuf[gi * NJ + j] - norm
-        for peer in z_peers:
-            remote(pbuf, pbuf, p_send, p_recv, peer)
-
-    for copy in (id_moved, c_moved, z_moved, stats_moved(0), stats_moved(1)):
-        copy.wait_send()
-
-    @pl.when(z != ROOT)
-    def _():
-        moved(lse, l_send, l_recv).wait_send()
-        moved(pbuf, p_send, p_recv).wait_recv()
-
-    @pl.when(z == ROOT)
-    def _():
-        v_moved.wait_send()
-        for _ in range(NZ - 1):
-            moved(pbuf, p_send, p_recv).wait_send()
-
-    posterior_out[...] = pbuf[...]
+        moved(vbuf.at[pl.ds(0, NZ - 1)], r_send, r_recv).wait_send()
 
 
 def finish(evidence, ess, posterior, evidence_out, ess_out, posterior_out, sem):
@@ -311,7 +315,6 @@
             vmem((EVENTS, 2, LANE), f32),
             vmem((NZ, 1, LANE), f32),
             vmem((NG * NJ, 1, LANE), f32),
-            vmem((NJ, LANE), f32),
             dma((5,)),
             dma((len(SIZES),)),
             dma, dma,

time: 37.6 us -> 37.7 us (level)
  the two profiles are of different devices: /device:TPU:1 before, /device:TPU:32 now
where the time goes in v6:
time: 37.7 us; the launch traced here: 37.5 us
  Pallas kernels  36.9 us (98%)
  between operations  0.64 us (2%)
    pallas_call x1, Pallas kernels, body(): pl.pallas_call(kernel, name='reweight', out_shape=(kept, kept, kept), in_...  36.3 us

profile of v6, /device:TPU:32, one launch (start us, length us, event | category | flops | bytes accessed | tf_op | source)
XLA Modules:
  0.0 37.5 jit_solution(4702881910410724535)
XLA Ops:
  0.6 36.3 %reweight.1 = (f32[4,128]{1,0:T(4,128)S(1)}, f32[4,128]{1,0:T(4,128)S(1)}, f32[4,128]{1,0:T(4,128)S(1)}) custom-call(bf16[2048,1024]{1,0:T(8,128)(2,1)} %summary.1, bf16[1024,512]{1,0:T(8,128)(2,1)} %weight.1, f32[16,128]{1,0:T(8,128)} %bitcast.5, f32[4,128]{1,0:T(4,128)} %bitcast.6, s32[16]{0:T(128)} %event_in.1, s32[16]{0:T(128)} %live_in.1), custom_call_target="tpu_custom_call" | custom-call | flops 2147483648 | bytes 4194304 | tf_op jit(solution)/shard_map/reweight/pallas_call | solution.py:294
  36.9 0.6 %finish.1 = (f32[4,128]{1,0:T(4,128)}, f32[4,128]{1,0:T(4,128)}, f32[4,128]{1,0:T(4,128)}) custom-call(f32[4,128]{1,0:T(4,128)S(1)} %get-tuple-element.9.evidence, f32[4,128]{1,0:T(4,128)S(1)} %get-tuple-element.10.ess, f32[4,128]{1,0:T(4,128)S(1)} %get-tuple-element.11.posterior), custom_call_target="tpu_custom_call" | custom-call | tf_op jit(solution)/shard_map/finish/pallas_call | solution.py:337

commit v7 on v6

--- a/solution.py
+++ b/solution.py
@@ -15,6 +15,7 @@
 SIZES = (256, 512, 512, 512, 256)
 WAITS = 3
 ROOT = 0
+DIRECT = 4
 HOP = 4
 BIG = -1e30
 LOG2E = 1.4426950408889634
@@ -27,7 +28,7 @@
     x_buf, w_buf, scores, prior_buf, offset_buf, event, live,
     yid, ysend, yrecv, held, lse, lse_all, zsend, zrecv, crecv, vbuf,
     in_sem, x_sem, id_send, id_recv, y_send, y_recv, c_send, c_recv, z_send, z_recv,
-    l_send, l_recv, v_send, v_recv, r_send, r_recv, known,
+    l_send, l_recv, v_send, v_recv, r_send, r_recv, d_send, d_recv, known,
 ):
     gi, si = lax.axis_index("grid"), lax.axis_index("samp")
     x, c = gi // NC, lax.rem(gi, NC)
@@ -207,9 +208,10 @@
     v_moved = moved(vbuf.at[pl.ds(0, NG * NJ - 1)], v_send, v_recv)
     row_moved = moved(vbuf.at[0], r_send, r_recv)
 
-    def send_plane():
-        for peer in v_peers:
-            remote(vbuf.at[own], vbuf.at[own], v_send, v_recv, peer)
+    def send_plane(target, peers, send_sem, recv_sem):
+        for grid, samp in peers:
+            samp = target * NY + lax.rem(samp, NY)
+            remote(vbuf.at[own], vbuf.at[own], send_sem, recv_sem, (grid, samp))
 
 
     @pl.when(z == ROOT)
@@ -225,14 +227,17 @@
             first += jnp.exp2((lse_all[k] - top) * LOG2E)
         line = jnp.sum(top + jnp.log(first), axis=0, keepdims=True)
         vbuf[own] = (line - logs) * (1.0 / EVENTS) + offset_buf[pl.ds(y, 1), :]
-        send_plane()
-        for d in sorted(range(1, NZ), key=lambda d: abs(d - NZ // 2)):
+        send_plane(ROOT, v_peers, v_send, v_recv)
+        send_plane(ROOT + 1, [*v_peers, (gi, si)], d_send, d_recv)
+        for d in range(DIRECT, NZ):
             remote(vbuf.at[own], vbuf.at[own], r_send, r_recv, z_peers[d - 1])
-
-    @pl.when(z != ROOT)
+        for target in range(ROOT + 2, ROOT + DIRECT):
+            send_plane(target, [*v_peers, (gi, si)], d_send, d_recv)
+
+    @pl.when(z >= DIRECT)
     def _():
         row_moved.wait_recv()
-        send_plane()
+        send_plane(z, v_peers, v_send, v_recv)
 
     count = jnp.full((1, LANE), jnp.sum(jnp.where(lane == si, count, 0.0)))
     z_moved.wait_recv()
@@ -250,7 +255,14 @@
         evidence_out[j : j + 1, :] = top + jnp.log(first) + shift
         ess_out[j : j + 1, :] = first * first / (second * count)
 
-    v_moved.wait_recv()
+    @pl.when((z > ROOT) & (z < DIRECT))
+    def _():
+        moved(vbuf, d_send, d_recv).wait_recv()
+
+    @pl.when((z == ROOT) | (z >= DIRECT))
+    def _():
+        v_moved.wait_recv()
+
     best = vbuf[0]
     for k in range(1, NG * NJ):
         best = jnp.maximum(best, vbuf[k])
@@ -262,7 +274,7 @@
     for j in range(NJ):
         posterior_out[j : j + 1, :] = vbuf[gi * NJ + j] - norm
 
-    for copy in (id_moved, c_moved, z_moved, v_moved, stats_moved(0), stats_moved(1)):
+    for copy in (id_moved, c_moved, z_moved, stats_moved(0), stats_moved(1)):
         copy.wait_send()
 
     @pl.when(z != ROOT)
@@ -271,7 +283,13 @@
 
     @pl.when(z == ROOT)
     def _():
-        moved(vbuf.at[pl.ds(0, NZ - 1)], r_send, r_recv).wait_send()
+        moved(vbuf.at[pl.ds(0, NZ - DIRECT)], r_send, r_recv).wait_send()
+        rows = zrecv.at[pl.ds(0, (DIRECT - 1) * NG * NJ // 2)]
+        moved(rows, d_send, d_recv).wait_send()
+
+    @pl.when((z == ROOT) | (z >= DIRECT))
+    def _():
+        v_moved.wait_send()
 
 
 def finish(evidence, ess, posterior, evidence_out, ess_out, posterior_out, sem):
@@ -320,7 +338,7 @@
             dma, dma,
             dma((2,)),
             dma((2,)),
-            dma, dma, dma, dma, dma, dma, dma, dma, dma, dma,
+            dma, dma, dma, dma, dma, dma, dma, dma, dma, dma, dma, dma,
             pltpu.SemaphoreType.REGULAR((2,)),
         ],
         compiler_params=pltpu.CompilerParams(

time: 37.7 us -> 36.7 us (0.973)
  the two profiles are of different devices: /device:TPU:32 before, /device:TPU:1 now
where the time goes in v7:
time: 36.7 us; the launch traced here: 36.4 us
  Pallas kernels  35.8 us (98%)
  between operations  0.64 us (2%)
    pallas_call x1, Pallas kernels, body(): pl.pallas_call(kernel, name='reweight', out_shape=(kept, kept, kept), in_...  35.2 us

profile of v7, /device:TPU:1, one launch (start us, length us, event | category | flops | bytes accessed | tf_op | source)
XLA Modules:
  0.0 36.4 jit_solution(313002052926257293)
XLA Ops:
  0.6 35.2 %reweight.1 = (f32[4,128]{1,0:T(4,128)S(1)}, f32[4,128]{1,0:T(4,128)S(1)}, f32[4,128]{1,0:T(4,128)S(1)}) custom-call(bf16[2048,1024]{1,0:T(8,128)(2,1)} %summary.1, bf16[1024,512]{1,0:T(8,128)(2,1)} %weight.1, f32[16,128]{1,0:T(8,128)} %bitcast.5, f32[4,128]{1,0:T(4,128)} %bitcast.6, s32[16]{0:T(128)} %event_in.1, s32[16]{0:T(128)} %live_in.1), custom_call_target="tpu_custom_call" | custom-call | flops 2147483648 | bytes 4194304 | tf_op jit(solution)/shard_map/reweight/pallas_call | solution.py:312
  35.8 0.6 %finish.1 = (f32[4,128]{1,0:T(4,128)}, f32[4,128]{1,0:T(4,128)}, f32[4,128]{1,0:T(4,128)}) custom-call(f32[4,128]{1,0:T(4,128)S(1)} %get-tuple-element.9.evidence, f32[4,128]{1,0:T(4,128)S(1)} %get-tuple-element.10.ess, f32[4,128]{1,0:T(4,128)S(1)} %get-tuple-element.11.posterior), custom_call_target="tpu_custom_call" | custom-call | tf_op jit(solution)/shard_map/finish/pallas_call | solution.py:355

commit v8 on v7

--- a/solution.py
+++ b/solution.py
@@ -15,7 +15,7 @@
 SIZES = (256, 512, 512, 512, 256)
 WAITS = 3
 ROOT = 0
-DIRECT = 4
+DIRECT = 5
 HOP = 4
 BIG = -1e30
 LOG2E = 1.4426950408889634

time: 36.7 us -> 36.6 us (level)
  no operation moved by 1% of the time
where the time goes in v8:
time: 36.6 us; the launch traced here: 36.4 us
  Pallas kernels  35.8 us (98%)
  between operations  0.64 us (2%)
    pallas_call x1, Pallas kernels, body(): pl.pallas_call(kernel, name='reweight', out_shape=(kept, kept, kept), in_...  35.2 us

profile of v8, /device:TPU:1, one launch (start us, length us, event | category | flops | bytes accessed | tf_op | source)
XLA Modules:
  0.0 36.4 jit_solution(6398543307974880153)
XLA Ops:
  0.6 35.2 %reweight.1 = (f32[4,128]{1,0:T(4,128)S(1)}, f32[4,128]{1,0:T(4,128)S(1)}, f32[4,128]{1,0:T(4,128)S(1)}) custom-call(bf16[2048,1024]{1,0:T(8,128)(2,1)} %summary.1, bf16[1024,512]{1,0:T(8,128)(2,1)} %weight.1, f32[16,128]{1,0:T(8,128)} %bitcast.5, f32[4,128]{1,0:T(4,128)} %bitcast.6, s32[16]{0:T(128)} %event_in.1, s32[16]{0:T(128)} %live_in.1), custom_call_target="tpu_custom_call" | custom-call | flops 2147483648 | bytes 4194304 | tf_op jit(solution)/shard_map/reweight/pallas_call | solution.py:312
  35.8 0.6 %finish.1 = (f32[4,128]{1,0:T(4,128)}, f32[4,128]{1,0:T(4,128)}, f32[4,128]{1,0:T(4,128)}) custom-call(f32[4,128]{1,0:T(4,128)S(1)} %get-tuple-element.9.evidence, f32[4,128]{1,0:T(4,128)S(1)} %get-tuple-element.10.ess, f32[4,128]{1,0:T(4,128)S(1)} %get-tuple-element.11.posterior), custom_call_target="tpu_custom_call" | custom-call | tf_op jit(solution)/shard_map/finish/pallas_call | solution.py:355
